TPU v7x, 32 devices: a whole 2x2x4 slice. The times are simulated.
32 devices in a mesh: gx: 4 (over z), gy: 4 (over x, core), gz: 2 (over y).
Axes of the slice: x: 2, y: 2, z: 4, core: 2. Of those that a mesh axis runs over, the one named last changes fastest.
Arguments:
- blocks: bfloat16 [4, 4, 128, 256, 256], P('gy', 'gx'), may hold values from -0.0625 to 0.0625
- block_rows: int32 [4, 4, 128], P('gy', 'gx'), may hold values from 0 to 15
- block_cols: int32 [4, 4, 128], P('gy', 'gx'), may hold values from 0 to 15
- probe_bits: int32 [16384, 256], P(('gy', 'gx'), 'gz'), may hold values from 0 to 1
- shift: float32 [16384], P(('gy', 'gx')), may hold values from 0 to 0.7
Outputs:
- forms: float32 [3, 256], P(None, 'gz')
- last_term: float32 [16384, 256], P(('gy', 'gx'), 'gz')
All inputs are finite; a program needn't handle non-finite values.
Results may differ from a plain program's by a relative error of at most 0.02.
Values may be sent and summed in bfloat16 or wider, within the bound.
No kernel may reach another device: no remote copies, remote signals or barrier semaphores. Data moves between devices by JAX's collectives and lax.ppermute only.
A program may use at most 128 MiB of HBM per device.

v0:
```python
import jax
import jax.numpy as jnp
from jax import lax
from jax.sharding import PartitionSpec as P


def body(blocks, block_rows, block_cols, probe_bits, shift):
    tile_blocks = blocks[0, 0]
    rows_here = block_rows[0, 0]
    cols_here = block_cols[0, 0]
    block_size = tile_blocks.shape[1]
    local_rows = shift.shape[0]
    probe_count = probe_bits.shape[1]
    tile_rows = local_rows // block_size * lax.axis_size("gx")
    signs = (2 * probe_bits - 1).astype(jnp.float32)

    def apply_operator(field):
        rounded = field.astype(jnp.bfloat16)
        whole = lax.all_gather(rounded, "gy", axis=0, tiled=True)
        whole = whole.reshape(whole.shape[0] // block_size, block_size, probe_count)
        picked = whole[cols_here]
        product = jnp.einsum(
            "kab,kbp->kap", tile_blocks, picked, preferred_element_type=jnp.float32
        )
        partial_rows = (
            jnp.zeros((tile_rows, block_size, probe_count), jnp.float32).at[rows_here].add(product)
        )
        summed = lax.psum_scatter(
            partial_rows.reshape(lax.axis_size("gx") * local_rows, probe_count).astype(
                jnp.bfloat16
            ),
            "gx",
            scatter_dimension=0,
            tiled=True,
        ).astype(jnp.float32)
        return summed + shift[:, None] * field

    first = apply_operator(signs)
    second = 2.0 * apply_operator(first) - signs
    third = 2.0 * apply_operator(second) - first
    forms = jnp.stack(
        [lax.psum(jnp.sum(signs * term, axis=0), ("gx", "gy")) for term in (first, second, third)]
    )
    return (forms, third)


def solution(mesh):
    return jax.shard_map(
        body,
        mesh=mesh,
        in_specs=(
            P("gy", "gx", None, None, None),
            P("gy", "gx", None),
            P("gy", "gx", None),
            P(("gy", "gx"), "gz"),
            P(("gy", "gx")),
        ),
        out_specs=(P(None, "gz"), P(("gy", "gx"), "gz")),
        check_vma=False,
    )
```

profile of v0, /device:TPU:0, one launch (start us, length us, event | category | flops | bytes accessed | tf_op | source)
XLA Modules:
  0.0 390.8 jit_solution(4236453247020909070)
XLA Ops:
  7.2 1.8 convert_convert_fusion
  9.1 0.7 fusion.18
  9.8 0.7 fusion.17
  10.4 19.1 %all-gather.4.cloned.1.call-done = bf16[4096,128]{1,0:T(8,128)(2,1)} async-done(((bf16[1024,128]{1,0:T(8,128)(2,1)}), bf16[4096,128]{1,0:T(8,128)(2,1)}) %all-gather.4.cloned.1.call-update) | async-done | bytes 1048592 | tf_op jit(solution)/shard_map/all_gather | solution.py:19
  29.6 7.8 %gather_fusion = bf16[128,256,128]{2,1,0:T(8,128)(2,1)} fusion(bf16[16,256,128]{2,1,0:T(8,128)(2,1)} %bitcast.39, s32[1024]{0:T(1024)S(1)} %pad_clamp_fusion), kind=kCustom, calls=%fused_computation | custom fusion | bytes 16777728 | tf_op jit(solution)/shard_map/gather | solution.py:21
  37.3 17.2 %fusion.6 = f32[128,256,128]{1,2,0:T(8,128)} fusion(bf16[128,256,128]{2,1,0:T(8,128)(2,1)} %gather_fusion, bf16[1,1,128,256,256]{4,3,2,1,0:T(8,128)(2,1)} %param.5), kind=kOutput, calls=%fused_computation.12 | convolution fusion | flops 2147483648 | bytes 41943040 | tf_op jit(solution)/shard_map/kab,kbp->kap/dot_general | solution.py:22
  54.5 17.4 %copy.11 = f32[128,256,128]{2,1,0:T(8,128)} copy(f32[128,256,128]{1,2,0:T(8,128)} %fusion.6) | data formatting | bytes 33554432 | tf_op jit(solution)/shard_map/kab,kbp->kap/dot_general | solution.py:22
  71.9 0.2 broadcast.45.clone
  72.1 24.3 %scatter_fusion = f32[16,256,128]{2,1,0:T(8,128)S(1)} fusion(f32[16,256,128]{2,1,0:T(8,128)S(1)} %broadcast.45.clone, s32[128]{0:T(128)S(1)} %fusion.17, f32[128,256,128]{2,1,0:T(8,128)} %copy.11), kind=kCustom, calls=%fused_computation.3 | custom fusion | flops 4194304 | bytes 50332160 | tf_op jit(solution)/shard_map/scatter-add | solution.py:26
  96.5 1.2 convert_element_type.41
  97.7 27.4 %reduce-scatter.4.cloned.1.call-done = bf16[1024,128]{1,0:T(8,128)(2,1)} async-done(((bf16[4096,128]{1,0:T(8,128)(2,1)}), bf16[1024,128]{1,0:T(8,128)(2,1)}) %reduce-scatter.4.cloned.1.call-update) | async-done | bytes 262160 | tf_op jit(solution)/shard_map/reduce_scatter | solution.py:28
  125.2 1.9 fusion.15
  127.1 15.4 %all-gather.6.cloned.1.call-done = bf16[4096,128]{1,0:T(8,128)(2,1)} async-done(((bf16[1024,128]{1,0:T(8,128)(2,1)}), bf16[4096,128]{1,0:T(8,128)(2,1)}) %all-gather.6.cloned.1.call-update) | async-done | bytes 1048592 | tf_op jit(solution)/shard_map/all_gather | solution.py:19
  142.5 7.8 %gather_fusion.1 = bf16[128,256,128]{2,1,0:T(8,128)(2,1)} fusion(bf16[16,256,128]{2,1,0:T(8,128)(2,1)} %bitcast.41, s32[1024]{0:T(1024)S(1)} %pad_clamp_fusion), kind=kCustom, calls=%fused_computation.1 | custom fusion | bytes 16777728 | tf_op jit(solution)/shard_map/gather | solution.py:21
  150.3 17.2 %fusion.9 = f32[128,256,128]{1,2,0:T(8,128)} fusion(bf16[128,256,128]{2,1,0:T(8,128)(2,1)} %gather_fusion.1, bf16[1,1,128,256,256]{4,3,2,1,0:T(8,128)(2,1)} %param.5), kind=kOutput, calls=%fused_computation.13 | convolution fusion | flops 2147483648 | bytes 41943040 | tf_op jit(solution)/shard_map/kab,kbp->kap/dot_general | solution.py:22
  167.5 17.4 %copy.13 = f32[128,256,128]{2,1,0:T(8,128)} copy(f32[128,256,128]{1,2,0:T(8,128)} %fusion.9) | data formatting | bytes 33554432 | tf_op jit(solution)/shard_map/kab,kbp->kap/dot_general | solution.py:22
  184.9 0.2 broadcast.45.clone.1
  185.1 24.3 %scatter_fusion.1 = f32[16,256,128]{2,1,0:T(8,128)S(1)} fusion(f32[16,256,128]{2,1,0:T(8,128)S(1)} %broadcast.45.clone.1, s32[128]{0:T(128)S(1)} %fusion.17, f32[128,256,128]{2,1,0:T(8,128)} %copy.13), kind=kCustom, calls=%fused_computation.4 | custom fusion | flops 4194304 | bytes 50332160 | tf_op jit(solution)/shard_map/scatter-add | solution.py:26
  209.4 1.2 convert_element_type.45
  210.7 27.4 %reduce-scatter.6.cloned.1.call-done = bf16[1024,128]{1,0:T(8,128)(2,1)} async-done(((bf16[4096,128]{1,0:T(8,128)(2,1)}), bf16[1024,128]{1,0:T(8,128)(2,1)}) %reduce-scatter.6.cloned.1.call-update) | async-done | bytes 262160 | tf_op jit(solution)/shard_map/reduce_scatter | solution.py:28
  238.1 1.9 fusion.16
  240.1 0.2 reduce-scatter.8.cloned.1.call-start
  240.3 15.1 %all-gather.8.cloned.1.call-done = bf16[4096,128]{1,0:T(8,128)(2,1)} async-done(((bf16[1024,128]{1,0:T(8,128)(2,1)}), bf16[4096,128]{1,0:T(8,128)(2,1)}) %all-gather.8.cloned.1.call-update) | async-done | bytes 1048592 | tf_op jit(solution)/shard_map/all_gather | solution.py:19
  255.4 7.8 %gather_fusion.2 = bf16[128,256,128]{2,1,0:T(8,128)(2,1)} fusion(bf16[16,256,128]{2,1,0:T(8,128)(2,1)} %bitcast.40, s32[1024]{0:T(1024)S(1)} %pad_clamp_fusion), kind=kCustom, calls=%fused_computation.2 | custom fusion | bytes 16777728 | tf_op jit(solution)/shard_map/gather | solution.py:21
  263.2 17.2 %fusion.12 = f32[128,256,128]{1,2,0:T(8,128)} fusion(bf16[128,256,128]{2,1,0:T(8,128)(2,1)} %gather_fusion.2, bf16[1,1,128,256,256]{4,3,2,1,0:T(8,128)(2,1)} %param.5), kind=kOutput, calls=%fused_computation.14 | convolution fusion | flops 2147483648 | bytes 41943040 | tf_op jit(solution)/shard_map/kab,kbp->kap/dot_general | solution.py:22
  280.4 17.4 %copy.15 = f32[128,256,128]{2,1,0:T(8,128)} copy(f32[128,256,128]{1,2,0:T(8,128)} %fusion.12) | data formatting | bytes 33554432 | tf_op jit(solution)/shard_map/kab,kbp->kap/dot_general | solution.py:22
  298.0 24.3 %scatter_fusion.2 = f32[16,256,128]{2,1,0:T(8,128)S(1)} fusion(f32[16,256,128]{2,1,0:T(8,128)S(1)} %broadcast.45, s32[128]{0:T(128)S(1)} %fusion.17, f32[128,256,128]{2,1,0:T(8,128)} %copy.15), kind=kCustom, calls=%fused_computation.5 | custom fusion | flops 4194304 | bytes 50332160 | tf_op jit(solution)/shard_map/scatter-add | solution.py:26
  322.3 1.2 convert_element_type.49
  323.5 27.5 %reduce-scatter.8.cloned.1.call-done = bf16[1024,128]{1,0:T(8,128)(2,1)} async-done(((bf16[4096,128]{1,0:T(8,128)(2,1)}), bf16[1024,128]{1,0:T(8,128)(2,1)}) %reduce-scatter.8.cloned.1.call-update) | async-done | bytes 262160 | tf_op jit(solution)/shard_map/reduce_scatter | solution.py:28
  351.0 2.2 multiply_reduce_fusion.2
  353.2 30.2 %all-reduce = (f32[1,128]{1,0:T(1,128)S(1)}, f32[1,128]{1,0:T(1,128)S(1)}, f32[1,128]{1,0:T(1,128)S(1)}) all-reduce(f32[1,128]{1,0:T(1,128)S(1)} %bitcast.47, f32[1,128]{1,0:T(1,128)S(1)} %bitcast.46, f32[1,128]{1,0:T(1,128)S(1)} %bitcast.45), channel_id=1, replica_groups=mesh['gx'=4,'gy'=4,'gz'=2] {'gx','gy'}, use_global_device_ids=true, to_apply=%region_11.0 | all-reduce | flops 384 | bytes 3072 | tf_op jit(solution)/shard_map/psum | solution.py:42
  383.4 0.6 pad_maximum_fusion
  (21 shorter events, 0.5 us)
Async XLA Ops:
  7.2 22.4 %all-gather.4.cloned.1.call-start = ((), (), s32[]{:S(2)}) async-start(), calls=%async_computation.3 | async-start | bytes 1310720 | tf_op jit(solution)/shard_map/all_gather | solution.py:19
  9.1 116.1 %reduce-scatter.4.cloned.1.call-start = ((), (), s32[]{:S(2)}) async-start(), calls=%async_computation.4 | async-start | bytes 1310720 | tf_op jit(solution)/shard_map/reduce_scatter | solution.py:28
  72.1 53.1 %copy-start = (s32[1024,128]{1,0:T(8,128)S(1)}, s32[1024,128]{1,0:T(8,128)}, u32[]{:S(2)}) copy-start(s32[1024,128]{1,0:T(8,128)} %param.8) | copy-start | bytes 1572868
  72.1 53.0 %copy-start.3 = (f32[1024]{0:T(1024)S(1)}, f32[1024]{0:T(1024)}, u32[]{:S(2)}) copy-start(f32[1024]{0:T(1024)} %param.9) | copy-start | bytes 12292
  97.7 44.9 %all-gather.6.cloned.1.call-start = ((), (), s32[]{:S(2)}) async-start(), calls=%async_computation.5 | async-start | bytes 1310720 | tf_op jit(solution)/shard_map/all_gather | solution.py:19
  127.1 111.1 %reduce-scatter.6.cloned.1.call-start = ((), (), s32[]{:S(2)}) async-start(), calls=%async_computation.6 | async-start | bytes 1310720 | tf_op jit(solution)/shard_map/reduce_scatter | solution.py:28
  185.1 53.0 %copy-start.1 = (bf16[1024,128]{1,0:T(8,128)(2,1)S(1)}, bf16[1024,128]{1,0:T(8,128)(2,1)}, u32[]{:S(2)}) copy-start(bf16[1024,128]{1,0:T(8,128)(2,1)} %reduce-scatter.4.cloned.1.call-done) | copy-start | bytes 786436
  210.6 44.8 %all-gather.8.cloned.1.call-start = ((), (), s32[]{:S(2)}) async-start(), calls=%async_computation.7 | async-start | bytes 1310720 | tf_op jit(solution)/shard_map/all_gather | solution.py:19
  240.1 110.9 %reduce-scatter.8.cloned.1.call-start = ((), (), s32[]{:S(2)}) async-start(), calls=%async_computation.8 | async-start | bytes 1310720 | tf_op jit(solution)/shard_map/reduce_scatter | solution.py:28
  298.0 53.0 %copy-start.2 = (bf16[1024,128]{1,0:T(8,128)(2,1)S(1)}, bf16[1024,128]{1,0:T(8,128)(2,1)}, u32[]{:S(2)}) copy-start(bf16[1024,128]{1,0:T(8,128)(2,1)} %reduce-scatter.6.cloned.1.call-done) | copy-start | bytes 786436
Sparse Core Ops, SparseCore 0:
  10.1 19.4 all-gather.3
  97.8 27.3 reduce-scatter.3
  127.3 15.1 all-gather.5
  210.7 27.3 reduce-scatter.5
  240.2 15.1 all-gather.7
  323.6 27.3 reduce-scatter.7
where the time goes:
time: 393 us; the launch traced here: 391 us
  waiting for transfers between devices  132 us (34%)
  other arithmetic  86.2 us (22%)
  local copies, waits for them, and re-layouts  76.1 us (19%)
  matrix products  51.5 us (13%)
  blocking collectives  30.2 us (8%)
  between operations  14.2 us (4%)
    reduce_scatter x3, waiting for transfers between devices, apply_operator(): lax.psum_scatter(partial_rows.reshape(lax.axis_size('gx') * local_rows, p...  82.4 us
    scatter-add x3, other arithmetic, apply_operator(): jnp.zeros((tile_rows, block_size, probe_count), jnp.float32).at[rows_here]  73 us
    dot_general x3, local copies, waits for them, and re-layouts, apply_operator(): jnp.einsum('kab,kbp->kap', tile_blocks, picked, preferred_element_type=jn...  52.2 us
    dot_general x3, matrix products, apply_operator(): jnp.einsum('kab,kbp->kap', tile_blocks, picked, preferred_element_type=jn...  51.5 us
    all_gather x3, waiting for transfers between devices, apply_operator(): whole = lax.all_gather(rounded, 'gy', axis=0, tiled=True)  49.7 us
    psum x1, blocking collectives, body(): lax.psum(jnp.sum(signs * term, axis=0), ('gx', 'gy'))  30.2 us
    gather x3, local copies, waits for them, and re-layouts, apply_operator(): picked = whole[cols_here]  23.3 us
  transfers between devices with their start and end apart: 6, of which 6 were waited for; matrix products, arithmetic and copies ran while one was open for 0% of the time, Pallas kernels for 0%

commit v1 on v0

v1 whole, which is shorter than its diff:
```python
import functools

import jax
import jax.numpy as jnp
from jax import lax
from jax.experimental import pallas as pl
from jax.experimental.pallas import tpu as pltpu
from jax.sharding import PartitionSpec as P

UNROLL = 8
VMEM = pl.BlockSpec(memory_space=pltpu.VMEM)
SMEM = pl.BlockSpec(memory_space=pltpu.SMEM)


def swap(value, axis, mask):
    n = lax.axis_size(axis)
    return lax.ppermute(value, axis, [(d, d ^ mask) for d in range(n)])


def multiply_kernel(pieces, slots, groups, plan_ref, blocks_ref, *refs):
    piece_refs = refs[:pieces]
    send_ref, keep_ref, field, total = refs[pieces:]
    size = blocks_ref.shape[1]
    rows = piece_refs[0].shape[0]
    for m, piece in enumerate(piece_refs):
        field[pl.ds(m * rows, rows), :] = piece[...]
    field[pl.ds(pieces * rows, size), :] = jnp.zeros((size, field.shape[1]), field.dtype)
    total[...] = jnp.zeros_like(total)

    def step(it, carry):
        for u in range(UNROLL):
            at = it * UNROLL + u
            col = plan_ref[1, at]
            row = plan_ref[2, at]
            part = jnp.dot(
                blocks_ref[plan_ref[0, at]],
                field[pl.ds(pl.multiple_of(col * size, size), size), :],
                preferred_element_type=jnp.float32,
            )
            total[row] += part
        return carry

    lax.fori_loop(0, plan_ref[3, 0], step, 0)
    half = total.shape[0] // 2
    keep_ref[...] = total[:half].reshape(keep_ref.shape)
    send_ref[...] = total[half:].reshape(send_ref.shape).astype(send_ref.dtype)


def make_plan(block_rows, block_cols, rb, n_gx, n_gy):
    kt = block_rows.shape[0]
    slots = kt + UNROLL
    here_x, here_y = lax.axis_index("gx"), lax.axis_index("gy")
    dest = (block_rows // rb) ^ here_x
    row = ((dest & 1) * (n_gx // 2) + dest // 2) * rb + block_rows % rb
    col = ((block_cols // rb) ^ here_y) * rb + block_cols % rb
    ids = jnp.arange(kt, dtype=jnp.int32)
    before = (row[None, :] > row[:, None]) | (
        (row[None, :] == row[:, None]) & (ids[None, :] < ids[:, None])
    )
    place = jnp.sum(before.astype(jnp.int32), axis=1)
    hit = place[None, :] == jnp.arange(slots, dtype=jnp.int32)[:, None]
    pick = lambda v, fill: jnp.sum(jnp.where(hit, v[None, :] - fill, 0), axis=1) + fill
    count = jnp.full((slots,), (kt + UNROLL - 1) // UNROLL, jnp.int32)
    return jnp.stack([pick(ids, 0), pick(col, n_gy * rb), pick(row, 0), count])


def body(blocks, block_rows, block_cols, probe_bits, shift):
    tile_blocks = blocks[0, 0]
    kt, size, _ = tile_blocks.shape
    local_rows, probes = probe_bits.shape
    rb = local_rows // size
    n_gx, n_gy = lax.axis_size("gx"), lax.axis_size("gy")
    plan = make_plan(block_rows[0, 0], block_cols[0, 0], rb, n_gx, n_gy)
    signs = (2 * probe_bits - 1).astype(jnp.float32)

    def apply_operator(field):
        pieces = [field.astype(jnp.bfloat16)]
        mask = n_gy // 2
        own = {0: pieces[0]}
        while mask:
            own.update({m | mask: swap(v, "gy", mask) for m, v in own.items()})
            mask //= 2
        pieces = [own[m] for m in range(n_gy)]
        half = n_gx // 2 * local_rows
        send, keep = pl.pallas_call(
            functools.partial(multiply_kernel, n_gy, plan.shape[1], 1),
            out_shape=(
                jax.ShapeDtypeStruct((half, probes), jnp.bfloat16),
                jax.ShapeDtypeStruct((half, probes), jnp.float32),
            ),
            in_specs=[SMEM, VMEM] + [VMEM] * n_gy,
            out_specs=(VMEM, VMEM),
            scratch_shapes=[
                pltpu.VMEM(((n_gy * rb + 1) * size, probes), jnp.bfloat16),
                pltpu.VMEM((n_gx * rb, size, probes), jnp.float32),
            ],
            compiler_params=pltpu.CompilerParams(vmem_limit_bytes=60 << 20),
            cost_estimate=pl.CostEstimate(
                flops=2 * kt * size * size * probes, bytes_accessed=kt * size * size * 2, transcendentals=0
            ),
            name="multiply",
        )(plan, tile_blocks, *pieces)
        mask, width = 1, n_gx // 2
        while True:
            keep = keep + swap(send, "gx", mask).astype(jnp.float32)
            mask *= 2
            if mask == n_gx:
                break
            parts = keep.reshape(width // 2, 2, local_rows, probes)
            send = parts[:, 1].reshape(-1, probes).astype(jnp.bfloat16)
            keep = parts[:, 0].reshape(-1, probes)
            width //= 2
        return keep + shift[:, None] * field

    first = apply_operator(signs)
    second = 2.0 * apply_operator(first) - signs
    third = 2.0 * apply_operator(second) - first
    forms = jnp.stack([jnp.sum(signs * term, axis=0) for term in (first, second, third)])
    for axis in ("gy", "gx"):
        mask = 1
        while mask < lax.axis_size(axis):
            forms = forms + swap(forms, axis, mask)
            mask *= 2
    return (forms, third)


def solution(mesh):
    return jax.shard_map(
        body,
        mesh=mesh,
        in_specs=(
            P("gy", "gx", None, None, None),
            P("gy", "gx", None),
            P("gy", "gx", None),
            P(("gy", "gx"), "gz"),
            P(("gy", "gx")),
        ),
        out_specs=(P(None, "gz"), P(("gy", "gx"), "gz")),
        check_vma=False,
    )
```

time: 393 us -> 182 us (0.46)
  other arithmetic: 86.2 us -> 8.95 us
  local copies, waits for them, and re-layouts: 76.1 us -> 2.3 us
  matrix products: 51.5 us -> 0 us
  Pallas kernels: 0 us -> 43.2 us
  waiting for transfers between devices: 132 us -> 101 us
  blocking collectives: 30.2 us -> 0 us
  starting transfers between devices: 0.43 us -> 25.5 us
  between operations: 14.2 us -> 0.82 us
    ppermute x0 -> x19, waiting for transfers between devices: none -> 101 us  [swap(): return lax.ppermute(value, axis, [(d, d ^ mask) for d in range(n)])]
    reduce_scatter x3 -> x0, waiting for transfers between devices: 82.4 us -> none  [apply_operator(): lax.psum_scatter(partial_rows.reshape(lax.axis_size('gx') * local_rows, p...]
    scatter-add x3 -> x0, other arithmetic: 73 us -> none  [apply_operator(): jnp.zeros((tile_rows, block_size, probe_count), jnp.float32).at[rows_here]]
    dot_general x3 -> x0, local copies, waits for them, and re-layouts: 52.2 us -> none  [apply_operator(): jnp.einsum('kab,kbp->kap', tile_blocks, picked, preferred_element_type=jn...]
    dot_general x3 -> x0, matrix products: 51.5 us -> none  [apply_operator(): jnp.einsum('kab,kbp->kap', tile_blocks, picked, preferred_element_type=jn...]
    all_gather x3 -> x0, waiting for transfers between devices: 49.7 us -> none  [apply_operator(): whole = lax.all_gather(rounded, 'gy', axis=0, tiled=True)]
    pallas_call x0 -> x3, Pallas kernels: none -> 43.2 us  [apply_operator(): pl.pallas_call(functools.partial(multiply_kernel, n_gy, plan.shape[1], 1)...]
    psum x1 -> x0, blocking collectives: 30.2 us -> none  [body(): lax.psum(jnp.sum(signs * term, axis=0), ('gx', 'gy'))]
  transfers between devices with their start and end apart: 6 -> 19, of which waited for: 6 -> 16; matrix products, arithmetic and copies ran while one was open for 0% -> 1% of each run, Pallas kernels for 0% -> 0%
where the time goes in v1:
time: 182 us
  waiting for transfers between devices  101 us (55%)
  Pallas kernels  43.2 us (24%)
  starting transfers between devices  25.5 us (14%)
  other arithmetic  8.95 us (5%)
  local copies, waits for them, and re-layouts  2.3 us (1%)
    ppermute x19, waiting for transfers between devices, swap(): return lax.ppermute(value, axis, [(d, d ^ mask) for d in range(n)])  101 us
    pallas_call x3, Pallas kernels, apply_operator(): pl.pallas_call(functools.partial(multiply_kernel, n_gy, plan.shape[1], 1)...  43.2 us
    ppermute x19, starting transfers between devices, swap(): return lax.ppermute(value, axis, [(d, d ^ mask) for d in range(n)])  25.5 us
    add x3, other arithmetic, apply_operator(): keep = keep + swap(send, 'gx', mask).astype(jnp.float32)  3.93 us
  transfers between devices with their start and end apart: 19, of which 16 were waited for; matrix products, arithmetic and copies ran while one was open for 1% of the time, Pallas kernels for 0%

profile of v1, /device:TPU:0, one launch (start us, length us, event | category | flops | bytes accessed | tf_op | source)
XLA Modules:
  0.0 181.9 jit_solution(442419534238915760)
XLA Ops:
  0.6 1.2 convert_convert_fusion.refs_0_
  1.8 3.0 %collective-permute-start.1 = (bf16[1024,128]{1,0:T(8,128)(2,1)S(1)}, bf16[1024,128]{1,0:T(8,128)(2,1)S(1)}, u32[]{:S(2)}, u32[]{:S(2)}) collective-permute-start(bf16[1024,128]{1,0:T(8,128)(2,1)S(1)} %convert_convert_fusion.refs_0_), channel_id=1, source_target_pairs={{0,4},{2,6},{4,0},{6,2},{1,5},{3,7},{5,1},{7,3},{8,12},{10,14},{12... | collective-permute-start | bytes 786440 | tf_op jit(solution)/shard_map/ppermute | solution.py:17
  5.9 5.2 %collective-permute-done.1.refs_2_ = bf16[1024,128]{1,0:T(8,128)(2,1)S(1)} collective-permute-done((bf16[1024,128]{1,0:T(8,128)(2,1)S(1)}, bf16[1024,128]{1,0:T(8,128)(2,1)S(1)}, u32[]{:S(2)}, u32[]{:S(2)}) %collective-permute-start.1) | collective-permute-done | bytes 262176 | tf_op jit(solution)/shard_map/ppermute | solution.py:17
  13.4 14.4 %multiply.3 = (bf16[2048,128]{1,0:T(8,128)(2,1)}, f32[2048,128]{1,0:T(8,128)}) custom-call(s32[4,136]{1,0:T(4,128)} %add_add_fusion.plan_ref, bf16[128,256,256]{2,1,0:T(8,128)(2,1)} %bitcast.74, bf16[1024,128]{1,0:T(8,128)(2,1)} %copy-done.1, bf16[1024,128]{1,0:T(8,128)(2,1)} %copy-done.5, bf16[1024,128]{1,0:T(8,128)(2,1)} %copy-done.4, ...), custom_call_target="tpu_custom_call" | custom-call | flops 2147483648 | bytes 16777216 | tf_op jit(solution)/shard_map/multiply/pallas_call | solution.py:85
  27.8 1.8 %collective-permute-start.3 = (bf16[2048,128]{1,0:T(8,128)(2,1)}, bf16[2048,128]{1,0:T(8,128)(2,1)S(1)}, u32[]{:S(2)}, u32[]{:S(2)}) collective-permute-start(bf16[2048,128]{1,0:T(8,128)(2,1)} %get-tuple-element.9), channel_id=1, source_target_pairs={{0,8},{8,0},{16,24},{24,16},{1,9},{9,1},{17,25},{25,17},{2,10},{10... | collective-permute-start | bytes 1572872 | tf_op jit(solution)/shard_map/ppermute | solution.py:17
  29.7 12.4 %collective-permute-done.3 = bf16[2048,128]{1,0:T(8,128)(2,1)S(1)} collective-permute-done((bf16[2048,128]{1,0:T(8,128)(2,1)}, bf16[2048,128]{1,0:T(8,128)(2,1)S(1)}, u32[]{:S(2)}, u32[]{:S(2)}) %collective-permute-start.3) | collective-permute-done | bytes 524320 | tf_op jit(solution)/shard_map/ppermute | solution.py:17
  42.1 1.3 convert_add_fusion.2
  43.4 2.8 %collective-permute-start.4 = (bf16[1024,128]{1,0:T(8,128)(2,1)S(1)}, bf16[1024,128]{1,0:T(8,128)(2,1)S(1)}, u32[]{:S(2)}, u32[]{:S(2)}) collective-permute-start(bf16[1024,128]{1,0:T(8,128)(2,1)S(1)} %fusion.10), channel_id=1, source_target_pairs={{0,16},{8,24},{16,0},{24,8},{1,17},{9,25},{17,1},{25,9},{2,18},{10... | collective-permute-start | bytes 786440 | tf_op jit(solution)/shard_map/ppermute | solution.py:17
  46.3 11.4 %collective-permute-done.4 = bf16[1024,128]{1,0:T(8,128)(2,1)S(1)} collective-permute-done((bf16[1024,128]{1,0:T(8,128)(2,1)S(1)}, bf16[1024,128]{1,0:T(8,128)(2,1)S(1)}, u32[]{:S(2)}, u32[]{:S(2)}) %collective-permute-start.4) | collective-permute-done | bytes 262176 | tf_op jit(solution)/shard_map/ppermute | solution.py:17
  57.9 1.6 collective-permute-start.6
  59.5 5.6 %collective-permute-done.6.refs_2_ = bf16[1024,128]{1,0:T(8,128)(2,1)S(1)} collective-permute-done((bf16[1024,128]{1,0:T(8,128)(2,1)S(1)}, bf16[1024,128]{1,0:T(8,128)(2,1)S(1)}, u32[]{:S(2)}, u32[]{:S(2)}) %collective-permute-start.6) | collective-permute-done | bytes 262176 | tf_op jit(solution)/shard_map/ppermute | solution.py:17
  65.1 1.5 collective-permute-done.7.refs_3_
  67.3 14.4 %multiply.4 = (bf16[2048,128]{1,0:T(8,128)(2,1)}, f32[2048,128]{1,0:T(8,128)}) custom-call(s32[4,136]{1,0:T(4,128)} %add_add_fusion.plan_ref, bf16[128,256,256]{2,1,0:T(8,128)(2,1)} %bitcast.75, bf16[1024,128]{1,0:T(8,128)(2,1)} %copy-done.3, bf16[1024,128]{1,0:T(8,128)(2,1)} %copy-done.10, bf16[1024,128]{1,0:T(8,128)(2,1)} %copy-done.8, ...), custom_call_target="tpu_custom_call" | custom-call | flops 2147483648 | bytes 16777216 | tf_op jit(solution)/shard_map/multiply/pallas_call | solution.py:85
  81.7 1.8 collective-permute-start.8
  83.5 12.4 %collective-permute-done.8 = bf16[2048,128]{1,0:T(8,128)(2,1)S(1)} collective-permute-done((bf16[2048,128]{1,0:T(8,128)(2,1)}, bf16[2048,128]{1,0:T(8,128)(2,1)S(1)}, u32[]{:S(2)}, u32[]{:S(2)}) %collective-permute-start.8) | collective-permute-done | bytes 524320 | tf_op jit(solution)/shard_map/ppermute | solution.py:17
  96.0 1.3 convert_add_fusion.1
  97.3 3.4 %collective-permute-start.9 = (bf16[1024,128]{1,0:T(8,128)(2,1)S(1)}, bf16[1024,128]{1,0:T(8,128)(2,1)S(1)}, u32[]{:S(2)}, u32[]{:S(2)}) collective-permute-start(bf16[1024,128]{1,0:T(8,128)(2,1)S(1)} %fusion.11), channel_id=1, source_target_pairs={{0,16},{8,24},{16,0},{24,8},{1,17},{9,25},{17,1},{25,9},{2,18},{10... | collective-permute-start | bytes 786440 | tf_op jit(solution)/shard_map/ppermute | solution.py:17
  100.8 11.6 %collective-permute-done.9 = bf16[1024,128]{1,0:T(8,128)(2,1)S(1)} collective-permute-done((bf16[1024,128]{1,0:T(8,128)(2,1)S(1)}, bf16[1024,128]{1,0:T(8,128)(2,1)S(1)}, u32[]{:S(2)}, u32[]{:S(2)}) %collective-permute-start.9) | collective-permute-done | bytes 262176 | tf_op jit(solution)/shard_map/ppermute | solution.py:17
  112.6 1.6 collective-permute-start.11
  114.2 5.8 %collective-permute-done.11.refs_2_ = bf16[1024,128]{1,0:T(8,128)(2,1)S(1)} collective-permute-done((bf16[1024,128]{1,0:T(8,128)(2,1)S(1)}, bf16[1024,128]{1,0:T(8,128)(2,1)S(1)}, u32[]{:S(2)}, u32[]{:S(2)}) %collective-permute-start.11) | collective-permute-done | bytes 262176 | tf_op jit(solution)/shard_map/ppermute | solution.py:17
  120.1 1.5 collective-permute-done.12.refs_3_
  122.3 14.4 %multiply.5 = (bf16[2048,128]{1,0:T(8,128)(2,1)}, f32[2048,128]{1,0:T(8,128)}) custom-call(s32[4,136]{1,0:T(4,128)} %add_add_fusion.plan_ref, bf16[128,256,256]{2,1,0:T(8,128)(2,1)} %bitcast.76, bf16[1024,128]{1,0:T(8,128)(2,1)} %copy-done.2, bf16[1024,128]{1,0:T(8,128)(2,1)} %copy-done.9, bf16[1024,128]{1,0:T(8,128)(2,1)} %copy-done.7, ...), custom_call_target="tpu_custom_call" | custom-call | flops 2147483648 | bytes 16777216 | tf_op jit(solution)/shard_map/multiply/pallas_call | solution.py:85
  136.7 1.6 collective-permute-start.13
  138.3 12.6 %collective-permute-done.13 = bf16[2048,128]{1,0:T(8,128)(2,1)S(1)} collective-permute-done((bf16[2048,128]{1,0:T(8,128)(2,1)}, bf16[2048,128]{1,0:T(8,128)(2,1)S(1)}, u32[]{:S(2)}, u32[]{:S(2)}) %collective-permute-start.13) | collective-permute-done | bytes 524320 | tf_op jit(solution)/shard_map/ppermute | solution.py:17
  150.9 1.3 convert_add_fusion
  152.2 3.3 %collective-permute-start.14 = (bf16[1024,128]{1,0:T(8,128)(2,1)S(1)}, bf16[1024,128]{1,0:T(8,128)(2,1)S(1)}, u32[]{:S(2)}, u32[]{:S(2)}) collective-permute-start(bf16[1024,128]{1,0:T(8,128)(2,1)S(1)} %fusion.12), channel_id=1, source_target_pairs={{0,16},{8,24},{16,0},{24,8},{1,17},{9,25},{17,1},{25,9},{2,18},{10... | collective-permute-start | bytes 786440 | tf_op jit(solution)/shard_map/ppermute | solution.py:17
  155.5 11.6 %collective-permute-done.14 = bf16[1024,128]{1,0:T(8,128)(2,1)S(1)} collective-permute-done((bf16[1024,128]{1,0:T(8,128)(2,1)S(1)}, bf16[1024,128]{1,0:T(8,128)(2,1)S(1)}, u32[]{:S(2)}, u32[]{:S(2)}) %collective-permute-start.14) | collective-permute-done | bytes 262176 | tf_op jit(solution)/shard_map/ppermute | solution.py:17
  169.5 1.6 collective-permute-start.16
  171.1 2.1 %collective-permute-done.16 = f32[3,128]{1,0:T(4,128)S(1)} collective-permute-done((f32[3,128]{1,0:T(4,128)S(1)}, f32[3,128]{1,0:T(4,128)S(1)}, u32[]{:S(2)}, u32[]{:S(2)}) %collective-permute-start.16) | collective-permute-done | bytes 1568 | tf_op jit(solution)/shard_map/ppermute | solution.py:17
  174.0 2.9 %collective-permute-done.17 = f32[3,128]{1,0:T(4,128)S(1)} collective-permute-done((f32[3,128]{1,0:T(4,128)S(1)}, f32[3,128]{1,0:T(4,128)S(1)}, u32[]{:S(2)}, u32[]{:S(2)}) %collective-permute-start.17) | collective-permute-done | bytes 1568 | tf_op jit(solution)/shard_map/ppermute | solution.py:17
  176.8 2.1 %collective-permute-start.18 = (f32[3,128]{1,0:T(4,128)S(1)}, f32[3,128]{1,0:T(4,128)S(1)}, u32[]{:S(2)}, u32[]{:S(2)}) collective-permute-start(f32[3,128]{1,0:T(4,128)S(1)} %add.158), channel_id=1, source_target_pairs={{0,16},{8,24},{16,0},{24,8},{1,17},{9,25},{17,1},{25,9},{2,18},{10... | collective-permute-start | bytes 4616 | tf_op jit(solution)/shard_map/ppermute | solution.py:17
  178.9 2.4 %collective-permute-done.18 = f32[3,128]{1,0:T(4,128)S(1)} collective-permute-done((f32[3,128]{1,0:T(4,128)S(1)}, f32[3,128]{1,0:T(4,128)S(1)}, u32[]{:S(2)}, u32[]{:S(2)}) %collective-permute-start.18) | collective-permute-done | bytes 1568 | tf_op jit(solution)/shard_map/ppermute | solution.py:17
  (58 shorter events, 8.9 us)
Async XLA Ops:
  0.6 57.0 %copy-start = (s32[1024,128]{1,0:T(8,128)S(1)}, s32[1024,128]{1,0:T(8,128)}, u32[]{:S(2)}) copy-start(s32[1024,128]{1,0:T(8,128)} %param.8) | copy-start | bytes 1572868
  0.6 57.0 %copy-start.13 = (f32[1024]{0:T(1024)S(1)}, f32[1024]{0:T(1024)}, u32[]{:S(2)}) copy-start(f32[1024]{0:T(1024)} %param.9) | copy-start | bytes 12292
  1.8 10.9 %copy-start.1 = (bf16[1024,128]{1,0:T(8,128)(2,1)}, bf16[1024,128]{1,0:T(8,128)(2,1)S(1)}, u32[]{:S(2)}) copy-start(bf16[1024,128]{1,0:T(8,128)(2,1)S(1)} %convert_convert_fusion.refs_0_) | copy-start | bytes 786436
  1.8 9.3 %collective-permute-start.1 = (bf16[1024,128]{1,0:T(8,128)(2,1)S(1)}, bf16[1024,128]{1,0:T(8,128)(2,1)S(1)}, u32[]{:S(2)}, u32[]{:S(2)}) collective-permute-start(bf16[1024,128]{1,0:T(8,128)(2,1)S(1)} %convert_convert_fusion.refs_0_), channel_id=1, source_target_pairs={{0,4},{2,6},{4,0},{6,2},{1,5},{3,7},{5,1},{7,3},{8,12},{10,14},{12... | collective-permute-start | bytes 786440 | tf_op jit(solution)/shard_map/ppermute | solution.py:17
  4.9 7.1 %collective-permute-start = (bf16[1024,128]{1,0:T(8,128)(2,1)S(1)}, bf16[1024,128]{1,0:T(8,128)(2,1)S(1)}, u32[]{:S(2)}, u32[]{:S(2)}) collective-permute-start(bf16[1024,128]{1,0:T(8,128)(2,1)S(1)} %convert_convert_fusion.refs_0_), channel_id=1, source_target_pairs={{0,2},{2,0},{4,6},{6,4},{1,3},{3,1},{5,7},{7,5},{8,10},{10,8},{12,... | collective-permute-start | bytes 786440 | tf_op jit(solution)/shard_map/ppermute | solution.py:17
  11.2 1.5 copy-start.4
  11.2 1.5 collective-permute-start.2
  11.9 0.8 copy-start.5
  27.8 14.3 %collective-permute-start.3 = (bf16[2048,128]{1,0:T(8,128)(2,1)}, bf16[2048,128]{1,0:T(8,128)(2,1)S(1)}, u32[]{:S(2)}, u32[]{:S(2)}) collective-permute-start(bf16[2048,128]{1,0:T(8,128)(2,1)} %get-tuple-element.9), channel_id=1, source_target_pairs={{0,8},{8,0},{16,24},{24,16},{1,9},{9,1},{17,25},{25,17},{2,10},{10... | collective-permute-start | bytes 1572872 | tf_op jit(solution)/shard_map/ppermute | solution.py:17
  43.4 14.2 %collective-permute-start.4 = (bf16[1024,128]{1,0:T(8,128)(2,1)S(1)}, bf16[1024,128]{1,0:T(8,128)(2,1)S(1)}, u32[]{:S(2)}, u32[]{:S(2)}) collective-permute-start(bf16[1024,128]{1,0:T(8,128)(2,1)S(1)} %fusion.10), channel_id=1, source_target_pairs={{0,16},{8,24},{16,0},{24,8},{1,17},{9,25},{17,1},{25,9},{2,18},{10... | collective-permute-start | bytes 786440 | tf_op jit(solution)/shard_map/ppermute | solution.py:17
  57.8 8.8 %copy-start.3 = (bf16[1024,128]{1,0:T(8,128)(2,1)}, bf16[1024,128]{1,0:T(8,128)(2,1)S(1)}, u32[]{:S(2)}) copy-start(bf16[1024,128]{1,0:T(8,128)(2,1)S(1)} %get-tuple-element.23.refs_0_) | copy-start | bytes 786436
  57.9 7.2 %collective-permute-start.6 = (bf16[1024,128]{1,0:T(8,128)(2,1)S(1)}, bf16[1024,128]{1,0:T(8,128)(2,1)S(1)}, u32[]{:S(2)}, u32[]{:S(2)}) collective-permute-start(bf16[1024,128]{1,0:T(8,128)(2,1)S(1)} %get-tuple-element.23.refs_0_), channel_id=1, source_target_pairs={{0,4},{2,6},{4,0},{6,2},{1,5},{3,7},{5,1},{7,3},{8,12},{10,14},{12... | collective-permute-start | bytes 786440 | tf_op jit(solution)/shard_map/ppermute | solution.py:17
  59.5 5.6 %collective-permute-start.5 = (bf16[1024,128]{1,0:T(8,128)(2,1)S(1)}, bf16[1024,128]{1,0:T(8,128)(2,1)S(1)}, u32[]{:S(2)}, u32[]{:S(2)}) collective-permute-start(bf16[1024,128]{1,0:T(8,128)(2,1)S(1)} %get-tuple-element.23.refs_0_), channel_id=1, source_target_pairs={{0,2},{2,0},{4,6},{6,4},{1,3},{3,1},{5,7},{7,5},{8,10},{10,8},{12,... | collective-permute-start | bytes 786440 | tf_op jit(solution)/shard_map/ppermute | solution.py:17
  65.1 1.5 copy-start.8
  65.1 1.5 collective-permute-start.7
  65.1 1.5 copy-start.10
  66.6 0.7 copy-start.12
  81.7 14.2 %collective-permute-start.8 = (bf16[2048,128]{1,0:T(8,128)(2,1)}, bf16[2048,128]{1,0:T(8,128)(2,1)S(1)}, u32[]{:S(2)}, u32[]{:S(2)}) collective-permute-start(bf16[2048,128]{1,0:T(8,128)(2,1)} %get-tuple-element.11), channel_id=1, source_target_pairs={{0,8},{8,0},{16,24},{24,16},{1,9},{9,1},{17,25},{25,17},{2,10},{10... | collective-permute-start | bytes 1572872 | tf_op jit(solution)/shard_map/ppermute | solution.py:17
  97.3 15.1 %collective-permute-start.9 = (bf16[1024,128]{1,0:T(8,128)(2,1)S(1)}, bf16[1024,128]{1,0:T(8,128)(2,1)S(1)}, u32[]{:S(2)}, u32[]{:S(2)}) collective-permute-start(bf16[1024,128]{1,0:T(8,128)(2,1)S(1)} %fusion.11), channel_id=1, source_target_pairs={{0,16},{8,24},{16,0},{24,8},{1,17},{9,25},{17,1},{25,9},{2,18},{10... | collective-permute-start | bytes 786440 | tf_op jit(solution)/shard_map/ppermute | solution.py:17
  112.6 8.9 %copy-start.2 = (bf16[1024,128]{1,0:T(8,128)(2,1)}, bf16[1024,128]{1,0:T(8,128)(2,1)S(1)}, u32[]{:S(2)}) copy-start(bf16[1024,128]{1,0:T(8,128)(2,1)S(1)} %get-tuple-element.21.refs_0_) | copy-start | bytes 786436
  112.6 7.4 %collective-permute-start.11 = (bf16[1024,128]{1,0:T(8,128)(2,1)S(1)}, bf16[1024,128]{1,0:T(8,128)(2,1)S(1)}, u32[]{:S(2)}, u32[]{:S(2)}) collective-permute-start(bf16[1024,128]{1,0:T(8,128)(2,1)S(1)} %get-tuple-element.21.refs_0_), channel_id=1, source_target_pairs={{0,4},{2,6},{4,0},{6,2},{1,5},{3,7},{5,1},{7,3},{8,12},{10,14},{12... | collective-permute-start | bytes 786440 | tf_op jit(solution)/shard_map/ppermute | solution.py:17
  114.2 5.8 %collective-permute-start.10 = (bf16[1024,128]{1,0:T(8,128)(2,1)S(1)}, bf16[1024,128]{1,0:T(8,128)(2,1)S(1)}, u32[]{:S(2)}, u32[]{:S(2)}) collective-permute-start(bf16[1024,128]{1,0:T(8,128)(2,1)S(1)} %get-tuple-element.21.refs_0_), channel_id=1, source_target_pairs={{0,2},{2,0},{4,6},{6,4},{1,3},{3,1},{5,7},{7,5},{8,10},{10,8},{12,... | collective-permute-start | bytes 786440 | tf_op jit(solution)/shard_map/ppermute | solution.py:17
  120.0 1.5 copy-start.7
  120.0 1.5 collective-permute-start.12
  120.0 1.5 copy-start.9
  121.6 0.7 copy-start.11
  136.7 14.2 %collective-permute-start.13 = (bf16[2048,128]{1,0:T(8,128)(2,1)}, bf16[2048,128]{1,0:T(8,128)(2,1)S(1)}, u32[]{:S(2)}, u32[]{:S(2)}) collective-permute-start(bf16[2048,128]{1,0:T(8,128)(2,1)} %get-tuple-element.13), channel_id=1, source_target_pairs={{0,8},{8,0},{16,24},{24,16},{1,9},{9,1},{17,25},{25,17},{2,10},{10... | collective-permute-start | bytes 1572872 | tf_op jit(solution)/shard_map/ppermute | solution.py:17
  152.2 15.0 %collective-permute-start.14 = (bf16[1024,128]{1,0:T(8,128)(2,1)S(1)}, bf16[1024,128]{1,0:T(8,128)(2,1)S(1)}, u32[]{:S(2)}, u32[]{:S(2)}) collective-permute-start(bf16[1024,128]{1,0:T(8,128)(2,1)S(1)} %fusion.12), channel_id=1, source_target_pairs={{0,16},{8,24},{16,0},{24,8},{1,17},{9,25},{17,1},{25,9},{2,18},{10... | collective-permute-start | bytes 786440 | tf_op jit(solution)/shard_map/ppermute | solution.py:17
  168.3 1.2 collective-permute-start.15
  169.5 3.7 %collective-permute-start.16 = (f32[3,128]{1,0:T(4,128)S(1)}, f32[3,128]{1,0:T(4,128)S(1)}, u32[]{:S(2)}, u32[]{:S(2)}) collective-permute-start(f32[3,128]{1,0:T(4,128)S(1)} %fusion.18), channel_id=1, source_target_pairs={{0,4},{2,6},{4,0},{6,2},{1,5},{3,7},{5,1},{7,3},{8,12},{10,14},{12... | collective-permute-start | bytes 4616 | tf_op jit(solution)/shard_map/ppermute | solution.py:17
  173.2 3.7 %collective-permute-start.17 = (f32[3,128]{1,0:T(4,128)S(1)}, f32[3,128]{1,0:T(4,128)S(1)}, u32[]{:S(2)}, u32[]{:S(2)}) collective-permute-start(f32[3,128]{1,0:T(4,128)S(1)} %fusion.24), channel_id=1, source_target_pairs={{0,8},{8,0},{16,24},{24,16},{1,9},{9,1},{17,25},{25,17},{2,10},{10... | collective-permute-start | bytes 4616 | tf_op jit(solution)/shard_map/ppermute | solution.py:17
  176.8 4.5 %collective-permute-start.18 = (f32[3,128]{1,0:T(4,128)S(1)}, f32[3,128]{1,0:T(4,128)S(1)}, u32[]{:S(2)}, u32[]{:S(2)}) collective-permute-start(f32[3,128]{1,0:T(4,128)S(1)} %add.158), channel_id=1, source_target_pairs={{0,16},{8,24},{16,0},{24,8},{1,17},{9,25},{17,1},{25,9},{2,18},{10... | collective-permute-start | bytes 4616 | tf_op jit(solution)/shard_map/ppermute | solution.py:17
  (1 other events, 0.7 us)

commit v2 on v0

v2 whole, which is shorter than its diff:
```python
import functools

import jax
import jax.numpy as jnp
from jax import lax
from jax.experimental import pallas as pl
from jax.experimental.pallas import tpu as pltpu
from jax.sharding import PartitionSpec as P


WIDE, NARROW = 16, 8
VMEM = pl.BlockSpec(memory_space=pltpu.VMEM)
ANY = pl.BlockSpec(memory_space=pl.ANY)
PARAMS = pltpu.CompilerParams(vmem_limit_bytes=24 << 20)


def swap(value, axis, mask):
    n = lax.axis_size(axis)
    return lax.ppermute(value, axis, [(d, d ^ mask) for d in range(n)])


def after(value, gate):
    return lax.optimization_barrier((value, gate))[0]


class Layout:
    def __init__(self, kt, size, probes, rb, n_gx, n_gy):
        self.kt, self.size, self.probes, self.rb, self.n_gx, self.n_gy = kt, size, probes, rb, n_gx, n_gy
        self.top, self.dests = n_gy // 2, n_gx // 2
        small = max(rb // 4, 1)
        self.chunks = [rb - rb // 2, rb // 2]
        self.starts = [sum(self.chunks[:c]) for c in range(len(self.chunks))]
        self.steps = (WIDE, WIDE, NARROW, NARROW)
        tail = self.chunks[-1]
        self.last = rb - tail
        self.fields = (self.top * self.last, self.top * rb, self.top * tail, self.top * tail)
        self.firsts = (0, 0, self.dests * rb, 0)
        self.slots = -(-(kt + sum(self.steps)) // 128) * 128

    def place(self, block_rows, block_cols):
        rb, here_x, here_y = self.rb, lax.axis_index("gx"), lax.axis_index("gy")
        dest, q = (block_rows // rb) ^ here_x, block_rows % rb
        piece, blk = (block_cols // rb) ^ here_y, block_cols % rb
        send = dest % 2
        row = send * (self.dests * rb)
        col = jnp.zeros_like(blk)
        for start, count in zip(self.starts, self.chunks):
            inside = (q >= start) & (q < start + count)
            row += jnp.where(inside, self.dests * start + dest // 2 * count + q - start, 0)
            inside = (blk >= start) & (blk < start + count)
            col += jnp.where(inside, self.top * start + piece % self.top * count + blk - start, 0)
        near, soon = piece < self.top, blk < self.last
        col -= jnp.where(near | soon, 0, self.top * self.last)
        which = jnp.where(near & soon, 0, jnp.where(near | soon, 1, 3 - send))
        return which, col, row


def start_kernel(lay, rows_hbm, cols_hbm, blocks_ref, held_ref, plan_ref, rows_ref, cols_ref, sem):
    kt, parts = lay.kt, sem.shape[0] - 2
    small = [
        pltpu.make_async_copy(rows_hbm, rows_ref, sem.at[parts]),
        pltpu.make_async_copy(cols_hbm, cols_ref, sem.at[parts + 1]),
    ]
    for copy in small:
        copy.start()
    cut = lambda ref, p: ref.at[pl.ds(p * (kt // parts), kt // parts)]
    copies = [pltpu.make_async_copy(cut(blocks_ref, p), cut(held_ref, p), sem.at[p]) for p in range(parts)]
    for copy in copies:
        copy.start()
    for copy in small:
        copy.wait()
    down, along = (lax.broadcasted_iota(jnp.int32, (kt, kt), d) for d in (0, 1))
    upright = lambda v: jnp.sum(jnp.where(down == along, v, 0), axis=1, keepdims=True)
    flat = lay.place(rows_ref[...], cols_ref[...])
    which, col, row = (upright(v) for v in flat)
    rank = jnp.sum(((flat[0] == which) & (along < down)).astype(jnp.int32), axis=1, keepdims=True)
    slots = lax.broadcasted_iota(jnp.int32, (1, lay.slots), 1)
    place, base = rank, jnp.zeros((1, 1), jnp.int32)
    fill_col, fill_row = jnp.zeros_like(slots), jnp.zeros_like(slots)
    sizes = jnp.zeros_like(slots)
    for number, step in enumerate(lay.steps):
        count = jnp.sum((flat[0] == number).astype(jnp.int32), axis=1, keepdims=True)
        trips = (count + step - 1) // step
        place += jnp.where(which == number, base, 0)
        end = base + trips * step
        inside = (slots >= base) & (slots < end)
        fill_col += jnp.where(inside, lay.fields[number], 0)
        fill_row += jnp.where(inside, lay.firsts[number], 0)
        sizes += jnp.where(slots == 2 * number, base, 0) + jnp.where(slots == 2 * number + 1, trips, 0)
        base = end
    hit = place == slots
    pick = lambda v: jnp.sum(jnp.where(hit, v, 0), axis=0, keepdims=True)
    empty = 1 - pick(1)
    plan_ref[0:1, :] = pick(lax.broadcasted_iota(jnp.int32, (kt, 1), 0))
    plan_ref[1:2, :] = pick(col) + empty * fill_col
    plan_ref[2:3, :] = pick(row) + empty * fill_row
    plan_ref[3:4, :] = sizes
    for copy in copies:
        copy.wait()


def run_list(lay, number, plan_hbm, blocks_ref, pieces, field, total, plan_ref, sem, prepare):
    size, first_row, step = lay.size, lay.firsts[number], lay.steps[number]
    fetch = pltpu.make_async_copy(plan_hbm, plan_ref, sem)
    fetch.start()
    prepare()
    place = 0
    for piece in pieces:
        field[pl.ds(place, piece.shape[0]), :] = piece[...]
        place += piece.shape[0]
    field[pl.ds(place, size), :] = jnp.zeros((size, lay.probes), field.dtype)
    fetch.wait()
    start = plan_ref[3, 2 * number]

    def go(it, carry):
        for u in range(step):
            at = start + it * step + u
            part = jnp.dot(
                blocks_ref[plan_ref[0, at]],
                field[pl.ds(pl.multiple_of(plan_ref[1, at] * size, size), size), :],
                preferred_element_type=jnp.float32,
            )
            total[plan_ref[2, at] - first_row] += part
        return carry

    lax.fori_loop(0, plan_ref[3, 2 * number + 1], go, 0)


def early_kernel(lay, number, plan_hbm, blocks_ref, *refs):
    before, refs = (refs[0], refs[1:]) if number else (None, refs)
    *pieces, total, field, plan_ref, sem = refs

    def prepare():
        total[...] = jnp.zeros_like(total) if before is None else before[...]

    run_list(lay, number, plan_hbm, blocks_ref, pieces, field, total, plan_ref, sem, prepare)


def late_kernel(lay, number, plan_hbm, blocks_ref, before, *refs):
    pieces, outs = refs[: lay.top], refs[lay.top : -4]
    field, total, plan_ref, sem = refs[-4:]

    def prepare():
        total[...] = before[pl.ds(lay.firsts[number], total.shape[0])]

    run_list(lay, number, plan_hbm, blocks_ref, pieces, field, total, plan_ref, sem, prepare)
    for out, start, count in zip(outs, lay.starts, lay.chunks):
        part = total[pl.ds(lay.dests * start, lay.dests * count)]
        out[...] = part.reshape(out.shape).astype(out.dtype)


def body(blocks, block_rows, block_cols, probe_bits, shift):
    kt, size, _ = blocks.shape[2:]
    local_rows, probes = probe_bits.shape
    n_gx, n_gy = lax.axis_size("gx"), lax.axis_size("gy")
    lay = Layout(kt, size, probes, local_rows // size, n_gx, n_gy)
    chunks = range(len(lay.chunks))

    def cost(share):
        return pl.CostEstimate(
            flops=int(2 * kt * size * size * probes * share), bytes_accessed=0, transcendentals=0
        )

    cut = lambda v: [v[s * size : (s + n) * size] for s, n in zip(lay.starts, lay.chunks)]
    signs = [(2 * v - 1).astype(jnp.float32) for v in cut(probe_bits)]
    scale = [v[:, None] for v in cut(shift)]

    begin = pl.pallas_call(
        functools.partial(start_kernel, lay),
        out_shape=(
            jax.ShapeDtypeStruct((kt, size, size), blocks.dtype),
            jax.ShapeDtypeStruct((4, lay.slots), jnp.int32),
        ),
        in_specs=[ANY, ANY, ANY],
        out_specs=(VMEM, VMEM),
        scratch_shapes=[
            pltpu.VMEM((1, kt), jnp.int32),
            pltpu.VMEM((1, kt), jnp.int32),
            pltpu.SemaphoreType.DMA((10,)),
        ],
        compiler_params=PARAMS,
        cost_estimate=cost(1.0),
        name="start",
    )
    held, plan = begin(block_rows[0], block_cols[0], blocks[0, 0])

    def spread(pieces):
        own, mask = {0: pieces}, lay.top // 2
        while mask:
            own.update({m | mask: swap(v, "gy", mask) for m, v in own.items()})
            mask //= 2
        return [own[m] for m in range(lay.top)]

    fetched = [pltpu.SMEM((4, lay.slots), jnp.int32), pltpu.SemaphoreType.DMA]

    def early(number, before, pieces, share):
        return pl.pallas_call(
            functools.partial(early_kernel, lay, number),
            out_shape=jax.ShapeDtypeStruct((n_gx * lay.rb, size, probes), jnp.float32),
            in_specs=[ANY, VMEM] + [VMEM] * (len(before) + len(pieces)),
            out_specs=VMEM,
            scratch_shapes=[pltpu.VMEM(((lay.fields[number] + 1) * size, probes), jnp.bfloat16)] + fetched,
            compiler_params=PARAMS,
            cost_estimate=cost(share),
        )(plan, held, *before, *pieces)

    def late(number, dtype, before, pieces, share):
        return pl.pallas_call(
            functools.partial(late_kernel, lay, number),
            out_shape=tuple(jax.ShapeDtypeStruct((lay.dests * n * size, probes), dtype) for n in lay.chunks),
            in_specs=[ANY, VMEM, VMEM] + [VMEM] * len(pieces),
            out_specs=(VMEM,) * len(lay.chunks),
            scratch_shapes=[
                pltpu.VMEM(((lay.fields[number] + 1) * size, probes), jnp.bfloat16),
                pltpu.VMEM((lay.dests * lay.rb, size, probes), jnp.float32),
            ]
            + fetched,
            compiler_params=PARAMS,
            cost_estimate=cost(share),
        )(plan, held, before, *pieces)

    def multiply(field):
        across = [swap(v, "gy", lay.top) for v in field]
        near = [spread(v) for v in field]
        far = [spread(v) for v in across[:-1]]
        total = early(0, [], sum(near[:-1], []), 0.25)
        total = early(1, [total], sum(far, []) + near[-1], 0.5)
        rest = spread(after(across[-1], total))
        send = late(2, jnp.bfloat16, total, rest, 0.12)
        return send, late(3, jnp.float32, total, rest, 0.12)

    def reduce(send, keep, gate=None):
        send, keep, last = list(send), list(keep), [None] * len(send)
        mask, width = 1, n_gx // 2
        while True:
            got = [swap(v, "gx", mask) for v in send]
            mask *= 2
            if mask == n_gx and gate is not None:
                sums = gate(last)
                got[0] = after(got[0], sums[0])
                got[-1] = after(got[-1], sums[1])
            for c in chunks:
                if c:
                    got[c] = after(got[c], send[c - 1] if mask < n_gx else keep[c - 1])
                keep[c] = keep[c] + got[c].astype(jnp.float32)
                if mask < n_gx:
                    parts = keep[c].reshape(width // 2, 2, -1, probes)
                    keep[c] = parts[:, 0].reshape(-1, probes)
                    gone = parts[:, 1].reshape(-1, probes)
                    last[c] = (keep[c], gone)
                    send[c] = gone.astype(jnp.bfloat16)
            width //= 2
            if mask == n_gx:
                return keep

    def apply_operator(field, previous, factor, gate=None):
        send, keep = multiply([v.astype(jnp.bfloat16) for v in field])
        sums = reduce(send, keep, gate)
        out = []
        for s, d, v, u in zip(sums, scale, field, previous):
            if out:
                s = after(s, out[-1].astype(jnp.bfloat16))
            term = factor * (s + d * v)
            out.append(term if u is None else term - u)
        return out

    def dot(us, vs):
        return sum(jnp.sum(u * v, axis=0) for u, v in zip(us, vs))

    far_signs = [swap(v.astype(jnp.bfloat16), "gx", n_gx // 2).astype(jnp.float32) for v in signs]
    first = apply_operator(signs, [None] * len(signs), 1.0)
    second = apply_operator(first, signs, 2.0)
    forms = []

    def add_forms(last):
        rest = [2.0 * d * v - u for d, v, u in zip(scale, second, first)]
        form3 = dot(signs, rest)
        form3 += 2.0 * (dot(signs, [v[0] for v in last]) + dot(far_signs, [v[1] for v in last]))
        total = jnp.stack([dot(signs, first), dot(signs, second), form3])
        mask, sums = 1, [total]
        while mask < n_gy:
            total = total + swap(total, "gy", mask)
            sums.append(total)
            mask *= 2
        total += sum(swap(total, "gx", m) for m in range(1, n_gx))
        forms.append(total)
        return sums[0], sums[-1]

    third = apply_operator(second, first, 2.0, add_forms)
    return (forms[0], jnp.concatenate(third))


def solution(mesh):
    return jax.shard_map(
        body,
        mesh=mesh,
        in_specs=(
            P("gy", "gx", None, None, None),
            P("gy", "gx", None),
            P("gy", "gx", None),
            P(("gy", "gx"), "gz"),
            P(("gy", "gx")),
        ),
        out_specs=(P(None, "gz"), P(("gy", "gx"), "gz")),
        check_vma=False,
    )
```

time: 393 us -> 142 us (0.36)
  other arithmetic: 86.2 us -> 4.26 us
  local copies, waits for them, and re-layouts: 76.1 us -> 1.41 us
  waiting for transfers between devices: 132 us -> 65.7 us
  matrix products: 51.5 us -> 0 us
  Pallas kernels: 0 us -> 37.2 us
  starting transfers between devices: 0.43 us -> 32.4 us
  blocking collectives: 30.2 us -> 0 us
  between operations: 14.2 us -> 1.08 us
    reduce_scatter x3 -> x0, waiting for transfers between devices: 82.4 us -> none  [apply_operator(): lax.psum_scatter(partial_rows.reshape(lax.axis_size('gx') * local_rows, p...]
    scatter-add x3 -> x0, other arithmetic: 73 us -> none  [apply_operator(): jnp.zeros((tile_rows, block_size, probe_count), jnp.float32).at[rows_here]]
    ppermute x0 -> x37, waiting for transfers between devices: none -> 65.7 us  [swap(): return lax.ppermute(value, axis, [(d, d ^ mask) for d in range(n)])]
    dot_general x3 -> x0, local copies, waits for them, and re-layouts: 52.2 us -> none  [apply_operator(): jnp.einsum('kab,kbp->kap', tile_blocks, picked, preferred_element_type=jn...]
    dot_general x3 -> x0, matrix products: 51.5 us -> none  [apply_operator(): jnp.einsum('kab,kbp->kap', tile_blocks, picked, preferred_element_type=jn...]
    all_gather x3 -> x0, waiting for transfers between devices: 49.7 us -> none  [apply_operator(): whole = lax.all_gather(rounded, 'gy', axis=0, tiled=True)]
    pallas_call x0 -> x13, Pallas kernels: none -> 37.2 us  [the longest x6 19.1 us: early(): pl.pallas_call(functools.partial(early_kernel, lay, number), out_shape=ja...]
    ppermute x0 -> x37, starting transfers between devices: none -> 32.4 us  [swap(): return lax.ppermute(value, axis, [(d, d ^ mask) for d in range(n)])]
  transfers between devices with their start and end apart: 6 -> 37, of which waited for: 6 -> 17; matrix products, arithmetic and copies ran while one was open for 0% -> 1% of each run, Pallas kernels for 0% -> 22%
where the time goes in v2:
time: 142 us
  waiting for transfers between devices  65.7 us (46%)
  Pallas kernels  37.2 us (26%)
  starting transfers between devices  32.4 us (23%)
  other arithmetic  4.26 us (3%)
    ppermute x37, waiting for transfers between devices, swap(): return lax.ppermute(value, axis, [(d, d ^ mask) for d in range(n)])  65.7 us
    ppermute x37, starting transfers between devices, swap(): return lax.ppermute(value, axis, [(d, d ^ mask) for d in range(n)])  32.4 us
    pallas_call x6, Pallas kernels, early(): pl.pallas_call(functools.partial(early_kernel, lay, number), out_shape=ja...  19.1 us
    pallas_call x6, Pallas kernels, late(): pl.pallas_call(functools.partial(late_kernel, lay, number), out_shape=tup...  12.1 us
    pallas_call x1, Pallas kernels, body(): held, plan = begin(block_rows[0], block_cols[0], blocks[0, 0])  5.94 us
  transfers between devices with their start and end apart: 37, of which 17 were waited for; matrix products, arithmetic and copies ran while one was open for 1% of the time, Pallas kernels for 22%

profile of v2, /device:TPU:0, one launch (start us, length us, event | category | flops | bytes accessed | tf_op | source)
XLA Modules:
  0.0 142.0 jit_solution(2110538083869807485)
XLA Ops:
  1.7 3.0 %collective-permute-start.1 = (bf16[512,128]{1,0:T(8,128)(2,1)S(1)}, bf16[512,128]{1,0:T(8,128)(2,1)S(1)}, u32[]{:S(2)}, u32[]{:S(2)}) collective-permute-start(bf16[512,128]{1,0:T(8,128)(2,1)S(1)} %get-tuple-element.78.refs_0_), channel_id=1, source_target_pairs={{0,4},{2,6},{4,0},{6,2},{1,5},{3,7},{5,1},{7,3},{8,12},{10,14},{12... | collective-permute-start | bytes 393224 | tf_op jit(solution)/shard_map/ppermute | solution.py:19
  5.4 3.3 %collective-permute-done.1.refs_1_ = bf16[512,128]{1,0:T(8,128)(2,1)S(1)} collective-permute-done((bf16[512,128]{1,0:T(8,128)(2,1)S(1)}, bf16[512,128]{1,0:T(8,128)(2,1)S(1)}, u32[]{:S(2)}, u32[]{:S(2)}) %collective-permute-start.1) | collective-permute-done | bytes 131104 | tf_op jit(solution)/shard_map/ppermute | solution.py:19
  10.0 5.9 %start.1 = (bf16[128,256,256]{2,1,0:T(8,128)(2,1)S(1)}, s32[4,256]{1,0:T(4,128)S(1)}) custom-call(s32[1,128]{1,0:T(1,128)S(1)} %bitcast.66, s32[1,128]{1,0:T(1,128)S(1)} %bitcast.67, bf16[128,256,256]{2,1,0:T(8,128)(2,1)} %bitcast.68), custom_call_target="tpu_custom_call" | custom-call | flops 2147483648 | tf_op jit(solution)/shard_map/start/pallas_call | solution.py:185
  15.9 2.1 %shard_map.68.refs_0_ = f32[16,256,128]{2,1,0:T(8,128)S(1)} custom-call(s32[4,256]{1,0:T(4,128)S(1)} %get-tuple-element.29.plan_hbm, bf16[128,256,256]{2,1,0:T(8,128)(2,1)S(1)} %get-tuple-element.30.blocks_ref, bf16[512,128]{1,0:T(8,128)(2,1)S(1)} %get-tuple-element.78.refs_0_, bf16[512,128]{1,0:T(8,128)(2,1)S(1)} %collective-permute-done.refs_1_), custom_call_target="tpu_custom_call" | custom-call | flops 536870912 | tf_op jit(solution)/shard_map/pallas_call | solution.py:197
  18.1 4.3 %shard_map.69.before = f32[16,256,128]{2,1,0:T(8,128)S(1)} custom-call(s32[4,256]{1,0:T(4,128)S(1)} %get-tuple-element.29.plan_hbm, bf16[128,256,256]{2,1,0:T(8,128)(2,1)S(1)} %get-tuple-element.30.blocks_ref, f32[16,256,128]{2,1,0:T(8,128)S(1)} %shard_map.68.refs_0_, bf16[512,128]{1,0:T(8,128)(2,1)S(1)} %collective-permute-done.1.refs_1_, ...), custom_call_target="tpu_custom_call" | custom-call | flops 1073741824 | tf_op jit(solution)/shard_map/pallas_call | solution.py:197
  23.8 2.0 %shard_map.71 = (bf16[1024,128]{1,0:T(8,128)(2,1)S(1)}, bf16[1024,128]{1,0:T(8,128)(2,1)S(1)}) custom-call(s32[4,256]{1,0:T(4,128)S(1)} %get-tuple-element.29.plan_hbm, bf16[128,256,256]{2,1,0:T(8,128)(2,1)S(1)} %get-tuple-element.30.blocks_ref, f32[16,256,128]{2,1,0:T(8,128)S(1)} %shard_map.69.before, bf16[512,128]{1,0:T(8,128)(2,1)S(1)} %collective-permute-done.4.refs_0_, ...), custom_call_target="tpu_custom_call" | custom-call | flops 257698032 | tf_op jit(solution)/shard_map/pallas_call | solution.py:208
  25.8 2.3 %collective-permute-start.6 = (bf16[1024,128]{1,0:T(8,128)(2,1)S(1)}, bf16[1024,128]{1,0:T(8,128)(2,1)S(1)}, u32[]{:S(2)}, u32[]{:S(2)}) collective-permute-start(bf16[1024,128]{1,0:T(8,128)(2,1)S(1)} %get-tuple-element.33), channel_id=1, source_target_pairs={{0,8},{8,0},{16,24},{24,16},{1,9},{9,1},{17,25},{25,17},{2,10},{10... | collective-permute-start | bytes 786440 | tf_op jit(solution)/shard_map/ppermute | solution.py:19
  28.2 2.0 %shard_map.70 = (f32[1024,128]{1,0:T(8,128)S(1)}, f32[1024,128]{1,0:T(8,128)S(1)}) custom-call(s32[4,256]{1,0:T(4,128)S(1)} %get-tuple-element.29.plan_hbm, bf16[128,256,256]{2,1,0:T(8,128)(2,1)S(1)} %get-tuple-element.30.blocks_ref, f32[16,256,128]{2,1,0:T(8,128)S(1)} %shard_map.69.before, bf16[512,128]{1,0:T(8,128)(2,1)S(1)} %collective-permute-done.4.refs_0_, ...), custom_call_target="tpu_custom_call" | custom-call | flops 257698032 | tf_op jit(solution)/shard_map/pallas_call | solution.py:208
  30.2 5.0 %collective-permute-done.6 = bf16[1024,128]{1,0:T(8,128)(2,1)S(1)} collective-permute-done((bf16[1024,128]{1,0:T(8,128)(2,1)S(1)}, bf16[1024,128]{1,0:T(8,128)(2,1)S(1)}, u32[]{:S(2)}, u32[]{:S(2)}) %collective-permute-start.6) | collective-permute-done | bytes 262176 | tf_op jit(solution)/shard_map/ppermute | solution.py:19
  35.3 2.6 %collective-permute-start.7 = (bf16[512,128]{1,0:T(8,128)(2,1)S(1)}, bf16[512,128]{1,0:T(8,128)(2,1)S(1)}, u32[]{:S(2)}, u32[]{:S(2)}) collective-permute-start(bf16[512,128]{1,0:T(8,128)(2,1)S(1)} %fusion.6), channel_id=1, source_target_pairs={{0,16},{8,24},{16,0},{24,8},{1,17},{9,25},{17,1},{25,9},{2,18},{10... | collective-permute-start | bytes 393224 | tf_op jit(solution)/shard_map/ppermute | solution.py:19
  38.0 5.4 %collective-permute-done.8 = bf16[1024,128]{1,0:T(8,128)(2,1)S(1)} collective-permute-done((bf16[1024,128]{1,0:T(8,128)(2,1)S(1)}, bf16[1024,128]{1,0:T(8,128)(2,1)S(1)}, u32[]{:S(2)}, u32[]{:S(2)}) %collective-permute-start.8) | collective-permute-done | bytes 262176 | tf_op jit(solution)/shard_map/ppermute | solution.py:19
  44.6 2.0 %collective-permute-start.11 = (bf16[512,128]{1,0:T(8,128)(2,1)S(1)}, bf16[512,128]{1,0:T(8,128)(2,1)S(1)}, u32[]{:S(2)}, u32[]{:S(2)}) collective-permute-start(bf16[512,128]{1,0:T(8,128)(2,1)S(1)} %get-tuple-element.74.refs_0_), channel_id=1, source_target_pairs={{0,4},{2,6},{4,0},{6,2},{1,5},{3,7},{5,1},{7,3},{8,12},{10,14},{12... | collective-permute-start | bytes 393224 | tf_op jit(solution)/shard_map/ppermute | solution.py:19
  46.6 5.8 %collective-permute-done.9 = bf16[512,128]{1,0:T(8,128)(2,1)S(1)} collective-permute-done((bf16[512,128]{1,0:T(8,128)(2,1)S(1)}, bf16[512,128]{1,0:T(8,128)(2,1)S(1)}, u32[]{:S(2)}, u32[]{:S(2)}) %collective-permute-start.9) | collective-permute-done | bytes 131104 | tf_op jit(solution)/shard_map/ppermute | solution.py:19
  54.6 2.1 %shard_map.72.refs_0_ = f32[16,256,128]{2,1,0:T(8,128)S(1)} custom-call(s32[4,256]{1,0:T(4,128)S(1)} %get-tuple-element.29.plan_hbm, bf16[128,256,256]{2,1,0:T(8,128)(2,1)S(1)} %get-tuple-element.30.blocks_ref, bf16[512,128]{1,0:T(8,128)(2,1)S(1)} %get-tuple-element.74.refs_0_, bf16[512,128]{1,0:T(8,128)(2,1)S(1)} %collective-permute-done.10.refs_1_), custom_call_target="tpu_custom_call" | custom-call | flops 536870912 | tf_op jit(solution)/shard_map/pallas_call | solution.py:197
  56.7 4.3 %shard_map.73.before = f32[16,256,128]{2,1,0:T(8,128)S(1)} custom-call(s32[4,256]{1,0:T(4,128)S(1)} %get-tuple-element.29.plan_hbm, bf16[128,256,256]{2,1,0:T(8,128)(2,1)S(1)} %get-tuple-element.30.blocks_ref, f32[16,256,128]{2,1,0:T(8,128)S(1)} %shard_map.72.refs_0_, bf16[512,128]{1,0:T(8,128)(2,1)S(1)} %collective-permute-done.11.refs_1_, ...), custom_call_target="tpu_custom_call" | custom-call | flops 1073741824 | tf_op jit(solution)/shard_map/pallas_call | solution.py:197
  62.4 2.0 %shard_map.75 = (bf16[1024,128]{1,0:T(8,128)(2,1)S(1)}, bf16[1024,128]{1,0:T(8,128)(2,1)S(1)}) custom-call(s32[4,256]{1,0:T(4,128)S(1)} %get-tuple-element.29.plan_hbm, bf16[128,256,256]{2,1,0:T(8,128)(2,1)S(1)} %get-tuple-element.30.blocks_ref, f32[16,256,128]{2,1,0:T(8,128)S(1)} %shard_map.73.before, bf16[512,128]{1,0:T(8,128)(2,1)S(1)} %collective-permute-done.14.refs_0_, ...), custom_call_target="tpu_custom_call" | custom-call | flops 257698032 | tf_op jit(solution)/shard_map/pallas_call | solution.py:208
  66.5 2.0 %shard_map.74 = (f32[1024,128]{1,0:T(8,128)S(1)}, f32[1024,128]{1,0:T(8,128)S(1)}) custom-call(s32[4,256]{1,0:T(4,128)S(1)} %get-tuple-element.29.plan_hbm, bf16[128,256,256]{2,1,0:T(8,128)(2,1)S(1)} %get-tuple-element.30.blocks_ref, f32[16,256,128]{2,1,0:T(8,128)S(1)} %shard_map.73.before, bf16[512,128]{1,0:T(8,128)(2,1)S(1)} %collective-permute-done.14.refs_0_, ...), custom_call_target="tpu_custom_call" | custom-call | flops 257698032 | tf_op jit(solution)/shard_map/pallas_call | solution.py:208
  68.5 5.1 %collective-permute-done.16 = bf16[1024,128]{1,0:T(8,128)(2,1)S(1)} collective-permute-done((bf16[1024,128]{1,0:T(8,128)(2,1)S(1)}, bf16[1024,128]{1,0:T(8,128)(2,1)S(1)}, u32[]{:S(2)}, u32[]{:S(2)}) %collective-permute-start.16) | collective-permute-done | bytes 262176 | tf_op jit(solution)/shard_map/ppermute | solution.py:19
  73.8 5.7 %collective-permute-done.18 = bf16[1024,128]{1,0:T(8,128)(2,1)S(1)} collective-permute-done((bf16[1024,128]{1,0:T(8,128)(2,1)S(1)}, bf16[1024,128]{1,0:T(8,128)(2,1)S(1)}, u32[]{:S(2)}, u32[]{:S(2)}) %collective-permute-start.18) | collective-permute-done | bytes 262176 | tf_op jit(solution)/shard_map/ppermute | solution.py:19
  83.0 4.6 %collective-permute-done.19 = bf16[512,128]{1,0:T(8,128)(2,1)S(1)} collective-permute-done((bf16[512,128]{1,0:T(8,128)(2,1)S(1)}, bf16[512,128]{1,0:T(8,128)(2,1)S(1)}, u32[]{:S(2)}, u32[]{:S(2)}) %collective-permute-start.19) | collective-permute-done | bytes 131104 | tf_op jit(solution)/shard_map/ppermute | solution.py:19
  89.3 2.1 %shard_map.76.refs_0_ = f32[16,256,128]{2,1,0:T(8,128)S(1)} custom-call(s32[4,256]{1,0:T(4,128)S(1)} %get-tuple-element.29.plan_hbm, bf16[128,256,256]{2,1,0:T(8,128)(2,1)S(1)} %get-tuple-element.30.blocks_ref, bf16[512,128]{1,0:T(8,128)(2,1)S(1)} %convert_element_type.111.refs_0_, bf16[512,128]{1,0:T(8,128)(2,1)S(1)} %collective-permute-done.20.refs_1_), custom_call_target="tpu_custom_call" | custom-call | flops 536870912 | tf_op jit(solution)/shard_map/pallas_call | solution.py:197
  91.4 4.3 %shard_map.77.before = f32[16,256,128]{2,1,0:T(8,128)S(1)} custom-call(s32[4,256]{1,0:T(4,128)S(1)} %get-tuple-element.29.plan_hbm, bf16[128,256,256]{2,1,0:T(8,128)(2,1)S(1)} %get-tuple-element.30.blocks_ref, f32[16,256,128]{2,1,0:T(8,128)S(1)} %shard_map.76.refs_0_, bf16[512,128]{1,0:T(8,128)(2,1)S(1)} %collective-permute-done.21.refs_1_, ...), custom_call_target="tpu_custom_call" | custom-call | flops 1073741824 | tf_op jit(solution)/shard_map/pallas_call | solution.py:197
  97.1 2.0 %shard_map.79 = (bf16[1024,128]{1,0:T(8,128)(2,1)S(1)}, bf16[1024,128]{1,0:T(8,128)(2,1)S(1)}) custom-call(s32[4,256]{1,0:T(4,128)S(1)} %get-tuple-element.29.plan_hbm, bf16[128,256,256]{2,1,0:T(8,128)(2,1)S(1)} %get-tuple-element.30.blocks_ref, f32[16,256,128]{2,1,0:T(8,128)S(1)} %shard_map.77.before, bf16[512,128]{1,0:T(8,128)(2,1)S(1)} %collective-permute-done.24.refs_0_, ...), custom_call_target="tpu_custom_call" | custom-call | flops 257698032 | tf_op jit(solution)/shard_map/pallas_call | solution.py:208
  100.4 2.1 %collective-permute-start.28 = (bf16[512,128]{1,0:T(8,128)(2,1)S(1)}, bf16[512,128]{1,0:T(8,128)(2,1)S(1)}, u32[]{:S(2)}, u32[]{:S(2)}) collective-permute-start(bf16[512,128]{1,0:T(8,128)(2,1)S(1)} %get-tuple-element.78.refs_0_), channel_id=1, source_target_pairs={{0,16},{8,24},{16,0},{24,8},{1,17},{9,25},{17,1},{25,9},{2,18},{10... | collective-permute-start | bytes 393224 | tf_op jit(solution)/shard_map/ppermute | solution.py:19
  104.2 2.0 %shard_map.78 = (f32[1024,128]{1,0:T(8,128)S(1)}, f32[1024,128]{1,0:T(8,128)S(1)}) custom-call(s32[4,256]{1,0:T(4,128)S(1)} %get-tuple-element.29.plan_hbm, bf16[128,256,256]{2,1,0:T(8,128)(2,1)S(1)} %get-tuple-element.30.blocks_ref, f32[16,256,128]{2,1,0:T(8,128)S(1)} %shard_map.77.before, bf16[512,128]{1,0:T(8,128)(2,1)S(1)} %collective-permute-done.24.refs_0_, ...), custom_call_target="tpu_custom_call" | custom-call | flops 257698032 | tf_op jit(solution)/shard_map/pallas_call | solution.py:208
  106.2 7.0 %collective-permute-done.26 = bf16[1024,128]{1,0:T(8,128)(2,1)S(1)} collective-permute-done((bf16[1024,128]{1,0:T(8,128)(2,1)S(1)}, bf16[1024,128]{1,0:T(8,128)(2,1)S(1)}, u32[]{:S(2)}, u32[]{:S(2)}) %collective-permute-start.26) | collective-permute-done | bytes 262176 | tf_op jit(solution)/shard_map/ppermute | solution.py:19
  113.3 5.0 %collective-permute-done.27 = bf16[1024,128]{1,0:T(8,128)(2,1)S(1)} collective-permute-done((bf16[1024,128]{1,0:T(8,128)(2,1)S(1)}, bf16[1024,128]{1,0:T(8,128)(2,1)S(1)}, u32[]{:S(2)}, u32[]{:S(2)}) %collective-permute-start.27) | collective-permute-done | bytes 262176 | tf_op jit(solution)/shard_map/ppermute | solution.py:19
  121.1 2.5 %collective-permute-done.31 = f32[3,128]{1,0:T(4,128)S(1)} collective-permute-done((f32[3,128]{1,0:T(4,128)S(1)}, f32[3,128]{1,0:T(4,128)S(1)}, u32[]{:S(2)}, u32[]{:S(2)}) %collective-permute-start.31) | collective-permute-done | bytes 1568 | tf_op jit(solution)/shard_map/ppermute | solution.py:19
  123.7 1.8 %collective-permute-start.34 = (f32[3,128]{1,0:T(4,128)S(1)}, f32[3,128]{1,0:T(4,128)S(1)}, u32[]{:S(2)}, u32[]{:S(2)}) collective-permute-start(f32[3,128]{1,0:T(4,128)S(1)} %fusion.16), channel_id=1, source_target_pairs={{0,24},{8,16},{16,8},{24,0},{1,25},{9,17},{17,9},{25,1},{2,26},{10... | collective-permute-start | bytes 4616 | tf_op jit(solution)/shard_map/ppermute | solution.py:19
  125.5 2.7 %collective-permute-start.33 = (f32[3,128]{1,0:T(4,128)S(1)}, f32[3,128]{1,0:T(4,128)S(1)}, u32[]{:S(2)}, u32[]{:S(2)}) collective-permute-start(f32[3,128]{1,0:T(4,128)S(1)} %fusion.16), channel_id=1, source_target_pairs={{0,16},{8,24},{16,0},{24,8},{1,17},{9,25},{17,1},{25,9},{2,18},{10... | collective-permute-start | bytes 4616 | tf_op jit(solution)/shard_map/ppermute | solution.py:19
  128.5 2.7 %collective-permute-start.36 = (bf16[512,128]{1,0:T(8,128)(2,1)S(1)}, bf16[512,128]{1,0:T(8,128)(2,1)S(1)}, u32[]{:S(2)}, u32[]{:S(2)}) collective-permute-start(bf16[512,128]{1,0:T(8,128)(2,1)S(1)} %fusion.5), channel_id=1, source_target_pairs={{0,16},{8,24},{16,0},{24,8},{1,17},{9,25},{17,1},{25,9},{2,18},{10... | collective-permute-start | bytes 393224 | tf_op jit(solution)/shard_map/ppermute | solution.py:19
  131.8 9.1 %collective-permute-done.36 = bf16[512,128]{1,0:T(8,128)(2,1)S(1)} collective-permute-done((bf16[512,128]{1,0:T(8,128)(2,1)S(1)}, bf16[512,128]{1,0:T(8,128)(2,1)S(1)}, u32[]{:S(2)}, u32[]{:S(2)}) %collective-permute-start.36) | collective-permute-done | bytes 131104 | tf_op jit(solution)/shard_map/ppermute | solution.py:19
  (95 shorter events, 26.1 us)
Async XLA Ops:
  1.7 6.9 %collective-permute-start.1 = (bf16[512,128]{1,0:T(8,128)(2,1)S(1)}, bf16[512,128]{1,0:T(8,128)(2,1)S(1)}, u32[]{:S(2)}, u32[]{:S(2)}) collective-permute-start(bf16[512,128]{1,0:T(8,128)(2,1)S(1)} %get-tuple-element.78.refs_0_), channel_id=1, source_target_pairs={{0,4},{2,6},{4,0},{6,2},{1,5},{3,7},{5,1},{7,3},{8,12},{10,14},{12... | collective-permute-start | bytes 393224 | tf_op jit(solution)/shard_map/ppermute | solution.py:19
  4.8 11.2 %collective-permute-start = (bf16[512,128]{1,0:T(8,128)(2,1)S(1)}, bf16[512,128]{1,0:T(8,128)(2,1)S(1)}, u32[]{:S(2)}, u32[]{:S(2)}) collective-permute-start(bf16[512,128]{1,0:T(8,128)(2,1)S(1)} %get-tuple-element.78.refs_0_), channel_id=1, source_target_pairs={{0,2},{2,0},{4,6},{6,4},{1,3},{3,1},{5,7},{7,5},{8,10},{10,8},{12,... | collective-permute-start | bytes 393224 | tf_op jit(solution)/shard_map/ppermute | solution.py:19
  4.8 13.3 %collective-permute-start.3 = (bf16[512,128]{1,0:T(8,128)(2,1)S(1)}, bf16[512,128]{1,0:T(8,128)(2,1)S(1)}, u32[]{:S(2)}, u32[]{:S(2)}) collective-permute-start(bf16[512,128]{1,0:T(8,128)(2,1)S(1)} %get-tuple-element.77.refs_3_), channel_id=1, source_target_pairs={{0,2},{2,0},{4,6},{6,4},{1,3},{3,1},{5,7},{7,5},{8,10},{10,8},{12,... | collective-permute-start | bytes 393224 | tf_op jit(solution)/shard_map/ppermute | solution.py:19
  5.3 17.1 %collective-permute-start.4 = (bf16[512,128]{1,0:T(8,128)(2,1)S(1)}, bf16[512,128]{1,0:T(8,128)(2,1)S(1)}, u32[]{:S(2)}, u32[]{:S(2)}) collective-permute-start(bf16[512,128]{1,0:T(8,128)(2,1)S(1)} %get-tuple-element.77.refs_3_), channel_id=1, source_target_pairs={{0,4},{2,6},{4,0},{6,2},{1,5},{3,7},{5,1},{7,3},{8,12},{10,14},{12... | collective-permute-start | bytes 393224 | tf_op jit(solution)/shard_map/ppermute | solution.py:19
  8.7 9.4 %collective-permute-start.2 = (bf16[512,128]{1,0:T(8,128)(2,1)S(1)}, bf16[512,128]{1,0:T(8,128)(2,1)S(1)}, u32[]{:S(2)}, u32[]{:S(2)}) collective-permute-start(bf16[512,128]{1,0:T(8,128)(2,1)S(1)} %collective-permute-done.1.refs_1_), channel_id=1, source_target_pairs={{0,2},{2,0},{4,6},{6,4},{1,3},{3,1},{5,7},{7,5},{8,10},{10,8},{12,... | collective-permute-start | bytes 393224 | tf_op jit(solution)/shard_map/ppermute | solution.py:19
  25.8 9.4 %collective-permute-start.6 = (bf16[1024,128]{1,0:T(8,128)(2,1)S(1)}, bf16[1024,128]{1,0:T(8,128)(2,1)S(1)}, u32[]{:S(2)}, u32[]{:S(2)}) collective-permute-start(bf16[1024,128]{1,0:T(8,128)(2,1)S(1)} %get-tuple-element.33), channel_id=1, source_target_pairs={{0,8},{8,0},{16,24},{24,16},{1,9},{9,1},{17,25},{25,17},{2,10},{10... | collective-permute-start | bytes 786440 | tf_op jit(solution)/shard_map/ppermute | solution.py:19
  28.1 15.2 %collective-permute-start.8 = (bf16[1024,128]{1,0:T(8,128)(2,1)S(1)}, bf16[1024,128]{1,0:T(8,128)(2,1)S(1)}, u32[]{:S(2)}, u32[]{:S(2)}) collective-permute-start(bf16[1024,128]{1,0:T(8,128)(2,1)S(1)} %get-tuple-element.35), channel_id=1, source_target_pairs={{0,8},{8,0},{16,24},{24,16},{1,9},{9,1},{17,25},{25,17},{2,10},{10... | collective-permute-start | bytes 786440 | tf_op jit(solution)/shard_map/ppermute | solution.py:19
  35.3 9.1 %collective-permute-start.7 = (bf16[512,128]{1,0:T(8,128)(2,1)S(1)}, bf16[512,128]{1,0:T(8,128)(2,1)S(1)}, u32[]{:S(2)}, u32[]{:S(2)}) collective-permute-start(bf16[512,128]{1,0:T(8,128)(2,1)S(1)} %fusion.6), channel_id=1, source_target_pairs={{0,16},{8,24},{16,0},{24,8},{1,17},{9,25},{17,1},{25,9},{2,18},{10... | collective-permute-start | bytes 393224 | tf_op jit(solution)/shard_map/ppermute | solution.py:19
  43.4 9.0 %collective-permute-start.9 = (bf16[512,128]{1,0:T(8,128)(2,1)S(1)}, bf16[512,128]{1,0:T(8,128)(2,1)S(1)}, u32[]{:S(2)}, u32[]{:S(2)}) collective-permute-start(bf16[512,128]{1,0:T(8,128)(2,1)S(1)} %fusion.7), channel_id=1, source_target_pairs={{0,16},{8,24},{16,0},{24,8},{1,17},{9,25},{17,1},{25,9},{2,18},{10... | collective-permute-start | bytes 393224 | tf_op jit(solution)/shard_map/ppermute | solution.py:19
  44.6 10.0 %collective-permute-start.10 = (bf16[512,128]{1,0:T(8,128)(2,1)S(1)}, bf16[512,128]{1,0:T(8,128)(2,1)S(1)}, u32[]{:S(2)}, u32[]{:S(2)}) collective-permute-start(bf16[512,128]{1,0:T(8,128)(2,1)S(1)} %get-tuple-element.74.refs_0_), channel_id=1, source_target_pairs={{0,2},{2,0},{4,6},{6,4},{1,3},{3,1},{5,7},{7,5},{8,10},{10,8},{12,... | collective-permute-start | bytes 393224 | tf_op jit(solution)/shard_map/ppermute | solution.py:19
  44.6 8.0 %collective-permute-start.11 = (bf16[512,128]{1,0:T(8,128)(2,1)S(1)}, bf16[512,128]{1,0:T(8,128)(2,1)S(1)}, u32[]{:S(2)}, u32[]{:S(2)}) collective-permute-start(bf16[512,128]{1,0:T(8,128)(2,1)S(1)} %get-tuple-element.74.refs_0_), channel_id=1, source_target_pairs={{0,4},{2,6},{4,0},{6,2},{1,5},{3,7},{5,1},{7,3},{8,12},{10,14},{12... | collective-permute-start | bytes 393224 | tf_op jit(solution)/shard_map/ppermute | solution.py:19
  52.6 4.1 %collective-permute-start.13 = (bf16[512,128]{1,0:T(8,128)(2,1)S(1)}, bf16[512,128]{1,0:T(8,128)(2,1)S(1)}, u32[]{:S(2)}, u32[]{:S(2)}) collective-permute-start(bf16[512,128]{1,0:T(8,128)(2,1)S(1)} %get-tuple-element.72.refs_3_), channel_id=1, source_target_pairs={{0,2},{2,0},{4,6},{6,4},{1,3},{3,1},{5,7},{7,5},{8,10},{10,8},{12,... | collective-permute-start | bytes 393224 | tf_op jit(solution)/shard_map/ppermute | solution.py:19
  52.7 4.0 %collective-permute-start.12 = (bf16[512,128]{1,0:T(8,128)(2,1)S(1)}, bf16[512,128]{1,0:T(8,128)(2,1)S(1)}, u32[]{:S(2)}, u32[]{:S(2)}) collective-permute-start(bf16[512,128]{1,0:T(8,128)(2,1)S(1)} %collective-permute-done.11.refs_1_), channel_id=1, source_target_pairs={{0,2},{2,0},{4,6},{6,4},{1,3},{3,1},{5,7},{7,5},{8,10},{10,8},{12,... | collective-permute-start | bytes 393224 | tf_op jit(solution)/shard_map/ppermute | solution.py:19
  53.1 7.8 %collective-permute-start.14 = (bf16[512,128]{1,0:T(8,128)(2,1)S(1)}, bf16[512,128]{1,0:T(8,128)(2,1)S(1)}, u32[]{:S(2)}, u32[]{:S(2)}) collective-permute-start(bf16[512,128]{1,0:T(8,128)(2,1)S(1)} %get-tuple-element.72.refs_3_), channel_id=1, source_target_pairs={{0,4},{2,6},{4,0},{6,2},{1,5},{3,7},{5,1},{7,3},{8,12},{10,14},{12... | collective-permute-start | bytes 393224 | tf_op jit(solution)/shard_map/ppermute | solution.py:19
  64.4 9.2 %collective-permute-start.16 = (bf16[1024,128]{1,0:T(8,128)(2,1)S(1)}, bf16[1024,128]{1,0:T(8,128)(2,1)S(1)}, u32[]{:S(2)}, u32[]{:S(2)}) collective-permute-start(bf16[1024,128]{1,0:T(8,128)(2,1)S(1)} %get-tuple-element.41), channel_id=1, source_target_pairs={{0,8},{8,0},{16,24},{24,16},{1,9},{9,1},{17,25},{25,17},{2,10},{10... | collective-permute-start | bytes 786440 | tf_op jit(solution)/shard_map/ppermute | solution.py:19
  64.7 14.8 %collective-permute-start.18 = (bf16[1024,128]{1,0:T(8,128)(2,1)S(1)}, bf16[1024,128]{1,0:T(8,128)(2,1)S(1)}, u32[]{:S(2)}, u32[]{:S(2)}) collective-permute-start(bf16[1024,128]{1,0:T(8,128)(2,1)S(1)} %get-tuple-element.43), channel_id=1, source_target_pairs={{0,8},{8,0},{16,24},{24,16},{1,9},{9,1},{17,25},{25,17},{2,10},{10... | collective-permute-start | bytes 786440 | tf_op jit(solution)/shard_map/ppermute | solution.py:19
  73.8 8.3 %collective-permute-start.17 = (bf16[512,128]{1,0:T(8,128)(2,1)S(1)}, bf16[512,128]{1,0:T(8,128)(2,1)S(1)}, u32[]{:S(2)}, u32[]{:S(2)}) collective-permute-start(bf16[512,128]{1,0:T(8,128)(2,1)S(1)} %fusion.8), channel_id=1, source_target_pairs={{0,16},{8,24},{16,0},{24,8},{1,17},{9,25},{17,1},{25,9},{2,18},{10... | collective-permute-start | bytes 393224 | tf_op jit(solution)/shard_map/ppermute | solution.py:19
  79.6 8.0 %collective-permute-start.19 = (bf16[512,128]{1,0:T(8,128)(2,1)S(1)}, bf16[512,128]{1,0:T(8,128)(2,1)S(1)}, u32[]{:S(2)}, u32[]{:S(2)}) collective-permute-start(bf16[512,128]{1,0:T(8,128)(2,1)S(1)} %fusion.9), channel_id=1, source_target_pairs={{0,16},{8,24},{16,0},{24,8},{1,17},{9,25},{17,1},{25,9},{2,18},{10... | collective-permute-start | bytes 393224 | tf_op jit(solution)/shard_map/ppermute | solution.py:19
  82.3 7.0 %collective-permute-start.20 = (bf16[512,128]{1,0:T(8,128)(2,1)S(1)}, bf16[512,128]{1,0:T(8,128)(2,1)S(1)}, u32[]{:S(2)}, u32[]{:S(2)}) collective-permute-start(bf16[512,128]{1,0:T(8,128)(2,1)S(1)} %convert_element_type.111.refs_0_), channel_id=1, source_target_pairs={{0,2},{2,0},{4,6},{6,4},{1,3},{3,1},{5,7},{7,5},{8,10},{10,8},{12,... | collective-permute-start | bytes 393224 | tf_op jit(solution)/shard_map/ppermute | solution.py:19
  82.4 5.9 %collective-permute-start.21 = (bf16[512,128]{1,0:T(8,128)(2,1)S(1)}, bf16[512,128]{1,0:T(8,128)(2,1)S(1)}, u32[]{:S(2)}, u32[]{:S(2)}) collective-permute-start(bf16[512,128]{1,0:T(8,128)(2,1)S(1)} %convert_element_type.111.refs_0_), channel_id=1, source_target_pairs={{0,4},{2,6},{4,0},{6,2},{1,5},{3,7},{5,1},{7,3},{8,12},{10,14},{12... | collective-permute-start | bytes 393224 | tf_op jit(solution)/shard_map/ppermute | solution.py:19
  87.8 3.7 %collective-permute-start.23 = (bf16[512,128]{1,0:T(8,128)(2,1)S(1)}, bf16[512,128]{1,0:T(8,128)(2,1)S(1)}, u32[]{:S(2)}, u32[]{:S(2)}) collective-permute-start(bf16[512,128]{1,0:T(8,128)(2,1)S(1)} %get-tuple-element.70.refs_3_), channel_id=1, source_target_pairs={{0,2},{2,0},{4,6},{6,4},{1,3},{3,1},{5,7},{7,5},{8,10},{10,8},{12,... | collective-permute-start | bytes 393224 | tf_op jit(solution)/shard_map/ppermute | solution.py:19
  88.3 7.4 %collective-permute-start.24 = (bf16[512,128]{1,0:T(8,128)(2,1)S(1)}, bf16[512,128]{1,0:T(8,128)(2,1)S(1)}, u32[]{:S(2)}, u32[]{:S(2)}) collective-permute-start(bf16[512,128]{1,0:T(8,128)(2,1)S(1)} %get-tuple-element.70.refs_3_), channel_id=1, source_target_pairs={{0,4},{2,6},{4,0},{6,2},{1,5},{3,7},{5,1},{7,3},{8,12},{10,14},{12... | collective-permute-start | bytes 393224 | tf_op jit(solution)/shard_map/ppermute | solution.py:19
  99.2 14.1 %collective-permute-start.26 = (bf16[1024,128]{1,0:T(8,128)(2,1)S(1)}, bf16[1024,128]{1,0:T(8,128)(2,1)S(1)}, u32[]{:S(2)}, u32[]{:S(2)}) collective-permute-start(bf16[1024,128]{1,0:T(8,128)(2,1)S(1)} %get-tuple-element.49), channel_id=1, source_target_pairs={{0,8},{8,0},{16,24},{24,16},{1,9},{9,1},{17,25},{25,17},{2,10},{10... | collective-permute-start | bytes 786440 | tf_op jit(solution)/shard_map/ppermute | solution.py:19
  99.5 18.9 %collective-permute-start.29 = (bf16[512,128]{1,0:T(8,128)(2,1)S(1)}, bf16[512,128]{1,0:T(8,128)(2,1)S(1)}, u32[]{:S(2)}, u32[]{:S(2)}) collective-permute-start(bf16[512,128]{1,0:T(8,128)(2,1)S(1)} %get-tuple-element.77.refs_3_), channel_id=1, source_target_pairs={{0,16},{8,24},{16,0},{24,8},{1,17},{9,25},{17,1},{25,9},{2,18},{10... | collective-permute-start | bytes 393224 | tf_op jit(solution)/shard_map/ppermute | solution.py:19
  100.4 18.1 %collective-permute-start.28 = (bf16[512,128]{1,0:T(8,128)(2,1)S(1)}, bf16[512,128]{1,0:T(8,128)(2,1)S(1)}, u32[]{:S(2)}, u32[]{:S(2)}) collective-permute-start(bf16[512,128]{1,0:T(8,128)(2,1)S(1)} %get-tuple-element.78.refs_0_), channel_id=1, source_target_pairs={{0,16},{8,24},{16,0},{24,8},{1,17},{9,25},{17,1},{25,9},{2,18},{10... | collective-permute-start | bytes 393224 | tf_op jit(solution)/shard_map/ppermute | solution.py:19
  102.5 15.9 %collective-permute-start.27 = (bf16[1024,128]{1,0:T(8,128)(2,1)S(1)}, bf16[1024,128]{1,0:T(8,128)(2,1)S(1)}, u32[]{:S(2)}, u32[]{:S(2)}) collective-permute-start(bf16[1024,128]{1,0:T(8,128)(2,1)S(1)} %get-tuple-element.51), channel_id=1, source_target_pairs={{0,8},{8,0},{16,24},{24,16},{1,9},{9,1},{17,25},{25,17},{2,10},{10... | collective-permute-start | bytes 786440 | tf_op jit(solution)/shard_map/ppermute | solution.py:19
  120.0 3.7 %collective-permute-start.31 = (f32[3,128]{1,0:T(4,128)S(1)}, f32[3,128]{1,0:T(4,128)S(1)}, u32[]{:S(2)}, u32[]{:S(2)}) collective-permute-start(f32[3,128]{1,0:T(4,128)S(1)} %fusion.10), channel_id=1, source_target_pairs={{0,4},{2,6},{4,0},{6,2},{1,5},{3,7},{5,1},{7,3},{8,12},{10,14},{12... | collective-permute-start | bytes 4616 | tf_op jit(solution)/shard_map/ppermute | solution.py:19
  123.7 7.5 %collective-permute-start.34 = (f32[3,128]{1,0:T(4,128)S(1)}, f32[3,128]{1,0:T(4,128)S(1)}, u32[]{:S(2)}, u32[]{:S(2)}) collective-permute-start(f32[3,128]{1,0:T(4,128)S(1)} %fusion.16), channel_id=1, source_target_pairs={{0,24},{8,16},{16,8},{24,0},{1,25},{9,17},{17,9},{25,1},{2,26},{10... | collective-permute-start | bytes 4616 | tf_op jit(solution)/shard_map/ppermute | solution.py:19
  125.5 5.7 %collective-permute-start.32 = (f32[3,128]{1,0:T(4,128)S(1)}, f32[3,128]{1,0:T(4,128)S(1)}, u32[]{:S(2)}, u32[]{:S(2)}) collective-permute-start(f32[3,128]{1,0:T(4,128)S(1)} %fusion.16), channel_id=1, source_target_pairs={{0,8},{8,0},{16,24},{24,16},{1,9},{9,1},{17,25},{25,17},{2,10},{10... | collective-permute-start | bytes 4616 | tf_op jit(solution)/shard_map/ppermute | solution.py:19
  125.5 5.7 %collective-permute-start.33 = (f32[3,128]{1,0:T(4,128)S(1)}, f32[3,128]{1,0:T(4,128)S(1)}, u32[]{:S(2)}, u32[]{:S(2)}) collective-permute-start(f32[3,128]{1,0:T(4,128)S(1)} %fusion.16), channel_id=1, source_target_pairs={{0,16},{8,24},{16,0},{24,8},{1,17},{9,25},{17,1},{25,9},{2,18},{10... | collective-permute-start | bytes 4616 | tf_op jit(solution)/shard_map/ppermute | solution.py:19
  128.2 12.7 %collective-permute-start.35 = (bf16[512,128]{1,0:T(8,128)(2,1)S(1)}, bf16[512,128]{1,0:T(8,128)(2,1)S(1)}, u32[]{:S(2)}, u32[]{:S(2)}) collective-permute-start(bf16[512,128]{1,0:T(8,128)(2,1)S(1)} %fusion.4), channel_id=1, source_target_pairs={{0,16},{8,24},{16,0},{24,8},{1,17},{9,25},{17,1},{25,9},{2,18},{10... | collective-permute-start | bytes 393224 | tf_op jit(solution)/shard_map/ppermute | solution.py:19
  128.5 12.4 %collective-permute-start.36 = (bf16[512,128]{1,0:T(8,128)(2,1)S(1)}, bf16[512,128]{1,0:T(8,128)(2,1)S(1)}, u32[]{:S(2)}, u32[]{:S(2)}) collective-permute-start(bf16[512,128]{1,0:T(8,128)(2,1)S(1)} %fusion.5), channel_id=1, source_target_pairs={{0,16},{8,24},{16,0},{24,8},{1,17},{9,25},{17,1},{25,9},{2,18},{10... | collective-permute-start | bytes 393224 | tf_op jit(solution)/shard_map/ppermute | solution.py:19
  (9 other events, 29.9 us)

commit v3 on v2

--- a/solution.py
+++ b/solution.py
@@ -9,8 +9,10 @@
 
 
 WIDE, NARROW = 16, 8
+PARTS, DEPTH = 16, 6
 VMEM = pl.BlockSpec(memory_space=pltpu.VMEM)
 ANY = pl.BlockSpec(memory_space=pl.ANY)
+HBM = pl.BlockSpec(memory_space=pltpu.HBM)
 PARAMS = pltpu.CompilerParams(vmem_limit_bytes=24 << 20)
 
 
@@ -55,23 +57,24 @@
         return which, col, row
 
 
-def start_kernel(lay, rows_hbm, cols_hbm, blocks_ref, held_ref, plan_ref, rows_ref, cols_ref, sem):
+def start_kernel(lay, tables_hbm, blocks_hbm, *refs):
+    pieces, (blocks_ref, plan_ref, total, tables_ref, field, planned, sem) = refs[:-7], refs[-7:]
     kt, parts = lay.kt, sem.shape[0] - 2
-    small = [
-        pltpu.make_async_copy(rows_hbm, rows_ref, sem.at[parts]),
-        pltpu.make_async_copy(cols_hbm, cols_ref, sem.at[parts + 1]),
-    ]
-    for copy in small:
-        copy.start()
-    cut = lambda ref, p: ref.at[pl.ds(p * (kt // parts), kt // parts)]
-    copies = [pltpu.make_async_copy(cut(blocks_ref, p), cut(held_ref, p), sem.at[p]) for p in range(parts)]
-    for copy in copies:
-        copy.start()
-    for copy in small:
-        copy.wait()
+    part = kt // parts
+
+    def copy(p):
+        cut = pl.ds(p * part, part)
+        return pltpu.make_async_copy(blocks_hbm.at[cut], blocks_ref.at[cut], sem.at[p])
+
+    tables = pltpu.make_async_copy(tables_hbm, tables_ref, sem.at[parts])
+    tables.start()
+    for p in range(DEPTH):
+        copy(p).start()
+    total[...] = jnp.zeros_like(total)
+    tables.wait()
     down, along = (lax.broadcasted_iota(jnp.int32, (kt, kt), d) for d in (0, 1))
     upright = lambda v: jnp.sum(jnp.where(down == along, v, 0), axis=1, keepdims=True)
-    flat = lay.place(rows_ref[...], cols_ref[...])
+    flat = lay.place(tables_ref[0:1, :], tables_ref[1:2, :])
     which, col, row = (upright(v) for v in flat)
     rank = jnp.sum(((flat[0] == which) & (along < down)).astype(jnp.int32), axis=1, keepdims=True)
     slots = lax.broadcasted_iota(jnp.int32, (1, lay.slots), 1)
@@ -95,11 +98,32 @@
     plan_ref[1:2, :] = pick(col) + empty * fill_col
     plan_ref[2:3, :] = pick(row) + empty * fill_row
     plan_ref[3:4, :] = sizes
-    for copy in copies:
-        copy.wait()
-
-
-def run_list(lay, number, plan_hbm, blocks_ref, pieces, field, total, plan_ref, sem, prepare):
+
+    def arrive(p, carry):
+        copy(p).wait()
+
+        @pl.when(p + DEPTH < parts)
+        def _():
+            copy(p + DEPTH).start()
+
+        return carry
+
+    def await_step(at, step, arrived):
+        need = planned[0, at]
+        for u in range(1, step):
+            need = jnp.maximum(need, planned[0, at + u])
+        need = jnp.maximum(need // part + 1, arrived)
+        lax.fori_loop(arrived, need, arrive, 0)
+        return need
+
+    def prepare():
+        pass
+
+    arrived = run_list(lay, 0, plan_ref, blocks_ref, pieces, field, total, planned, sem.at[parts + 1], prepare, await_step)
+    lax.fori_loop(arrived, parts, arrive, 0)
+
+
+def run_list(lay, number, plan_hbm, blocks_ref, pieces, field, total, plan_ref, sem, prepare, await_step=None):
     size, first_row, step = lay.size, lay.firsts[number], lay.steps[number]
     fetch = pltpu.make_async_copy(plan_hbm, plan_ref, sem)
     fetch.start()
@@ -113,6 +137,8 @@
     start = plan_ref[3, 2 * number]
 
     def go(it, carry):
+        if await_step:
+            carry = await_step(start + it * step, step, carry)
         for u in range(step):
             at = start + it * step + u
             part = jnp.dot(
@@ -123,7 +149,7 @@
             total[plan_ref[2, at] - first_row] += part
         return carry
 
-    lax.fori_loop(0, plan_ref[3, 2 * number + 1], go, 0)
+    return lax.fori_loop(0, plan_ref[3, 2 * number + 1], go, 0)
 
 
 def early_kernel(lay, number, plan_hbm, blocks_ref, *refs):
@@ -170,19 +196,22 @@
         out_shape=(
             jax.ShapeDtypeStruct((kt, size, size), blocks.dtype),
             jax.ShapeDtypeStruct((4, lay.slots), jnp.int32),
+            jax.ShapeDtypeStruct((n_gx * lay.rb, size, probes), jnp.float32),
         ),
-        in_specs=[ANY, ANY, ANY],
-        out_specs=(VMEM, VMEM),
+        in_specs=[ANY, ANY] + [VMEM] * (lay.top * (len(lay.chunks) - 1)),
+        out_specs=(VMEM, VMEM, VMEM),
         scratch_shapes=[
-            pltpu.VMEM((1, kt), jnp.int32),
-            pltpu.VMEM((1, kt), jnp.int32),
-            pltpu.SemaphoreType.DMA((10,)),
+            pltpu.VMEM((2, kt), jnp.int32),
+            pltpu.VMEM(((lay.fields[0] + 1) * size, probes), jnp.bfloat16),
+            pltpu.SMEM((4, lay.slots), jnp.int32),
+            pltpu.SemaphoreType.DMA((PARTS + 2,)),
         ],
         compiler_params=PARAMS,
         cost_estimate=cost(1.0),
         name="start",
     )
-    held, plan = begin(block_rows[0], block_cols[0], blocks[0, 0])
+    tables = jnp.concatenate([block_rows[0], block_cols[0]])
+    stored = []
 
     def spread(pieces):
         own, mask = {0: pieces}, lay.top // 2
@@ -202,7 +231,7 @@
             scratch_shapes=[pltpu.VMEM(((lay.fields[number] + 1) * size, probes), jnp.bfloat16)] + fetched,
             compiler_params=PARAMS,
             cost_estimate=cost(share),
-        )(plan, held, *before, *pieces)
+        )(*stored, *before, *pieces)
 
     def late(number, dtype, before, pieces, share):
         return pl.pallas_call(
@@ -217,15 +246,19 @@
             + fetched,
             compiler_params=PARAMS,
             cost_estimate=cost(share),
-        )(plan, held, before, *pieces)
-
-    def multiply(field):
+        )(*stored, before, *pieces)
+
+    def multiply(it, field):
         across = [swap(v, "gy", lay.top) for v in field]
         near = [spread(v) for v in field]
         far = [spread(v) for v in across[:-1]]
-        total = early(0, [], sum(near[:-1], []), 0.25)
+        if stored:
+            total = early(0, [], sum(near[:-1], []), 0.25)
+        else:
+            held, plan, total = begin(tables, blocks[0, 0], *sum(near[:-1], []))
+            stored.extend((plan, held))
         total = early(1, [total], sum(far, []) + near[-1], 0.5)
-        rest = spread(after(across[-1], total))
+        rest = spread(after(across[-1], total) if it else across[-1])
         send = late(2, jnp.bfloat16, total, rest, 0.12)
         return send, late(3, jnp.float32, total, rest, 0.12)
 
@@ -253,8 +286,8 @@
             if mask == n_gx:
                 return keep
 
-    def apply_operator(field, previous, factor, gate=None):
-        send, keep = multiply([v.astype(jnp.bfloat16) for v in field])
+    def apply_operator(it, field, previous, factor, gate=None):
+        send, keep = multiply(it, [v.astype(jnp.bfloat16) for v in field])
         sums = reduce(send, keep, gate)
         out = []
         for s, d, v, u in zip(sums, scale, field, previous):
@@ -267,9 +300,11 @@
     def dot(us, vs):
         return sum(jnp.sum(u * v, axis=0) for u, v in zip(us, vs))
 
-    far_signs = [swap(v.astype(jnp.bfloat16), "gx", n_gx // 2).astype(jnp.float32) for v in signs]
-    first = apply_operator(signs, [None] * len(signs), 1.0)
-    second = apply_operator(first, signs, 2.0)
+    far_signs = jnp.concatenate([v.astype(jnp.bfloat16) for v in signs])
+    far_signs = swap(far_signs, "gx", n_gx // 2)
+    far_signs = [v.astype(jnp.float32) for v in cut(far_signs)]
+    first = apply_operator(0, signs, [None] * len(signs), 1.0)
+    second = apply_operator(1, first, signs, 2.0)
     forms = []
 
     def add_forms(last):
@@ -282,11 +317,14 @@
             total = total + swap(total, "gy", mask)
             sums.append(total)
             mask *= 2
-        total += sum(swap(total, "gx", m) for m in range(1, n_gx))
+        mask = 1
+        while mask < n_gx:
+            total = total + swap(total, "gx", mask)
+            mask *= 2
         forms.append(total)
         return sums[0], sums[-1]
 
-    third = apply_operator(second, first, 2.0, add_forms)
+    third = apply_operator(2, second, first, 2.0, add_forms)
     return (forms[0], jnp.concatenate(third))
 
 

time: 142 us -> 136 us (0.958)
  starting transfers between devices: 32.4 us -> 27.1 us
    ppermute x37 -> x35, starting transfers between devices: 32.4 us -> 27.1 us  [swap(): return lax.ppermute(value, axis, [(d, d ^ mask) for d in range(n)])]
    pallas_call x6 -> x5, Pallas kernels: 19.1 us -> 17 us  [early(): pl.pallas_call(functools.partial(early_kernel, lay, number), out_shape=ja...]
    ppermute x37 -> x35, waiting for transfers between devices: 65.7 us -> 66.3 us  [swap(): return lax.ppermute(value, axis, [(d, d ^ mask) for d in range(n)])]
  transfers between devices with their start and end apart: 37 -> 35, of which waited for: 17 -> 17; matrix products, arithmetic and copies ran while one was open for 1% -> 2% of each run, Pallas kernels for 22% -> 22%
where the time goes in v3:
time: 136 us
  waiting for transfers between devices  66.3 us (49%)
  Pallas kernels  36.2 us (27%)
  starting transfers between devices  27.1 us (20%)
  other arithmetic  4.85 us (4%)
    ppermute x35, waiting for transfers between devices, swap(): return lax.ppermute(value, axis, [(d, d ^ mask) for d in range(n)])  66.3 us
    ppermute x35, starting transfers between devices, swap(): return lax.ppermute(value, axis, [(d, d ^ mask) for d in range(n)])  27.1 us
    pallas_call x5, Pallas kernels, early(): pl.pallas_call(functools.partial(early_kernel, lay, number), out_shape=ja...  17 us
    pallas_call x6, Pallas kernels, late(): pl.pallas_call(functools.partial(late_kernel, lay, number), out_shape=tup...  12.1 us
    pallas_call x1, Pallas kernels, multiply(): held, plan, total = begin(tables, blocks[0, 0], *sum(near[:-1], []))  7.06 us
  transfers between devices with their start and end apart: 35, of which 17 were waited for; matrix products, arithmetic and copies ran while one was open for 2% of the time, Pallas kernels for 22%

profile of v3, /device:TPU:0, one launch (start us, length us, event | category | flops | bytes accessed | tf_op | source)
XLA Modules:
  0.0 135.6 jit_solution(2523933996940752974)
XLA Ops:
  1.7 3.0 %collective-permute-start.1 = (bf16[512,128]{1,0:T(8,128)(2,1)S(1)}, bf16[512,128]{1,0:T(8,128)(2,1)S(1)}, u32[]{:S(2)}, u32[]{:S(2)}) collective-permute-start(bf16[512,128]{1,0:T(8,128)(2,1)S(1)} %get-tuple-element.78.refs_0_), channel_id=1, source_target_pairs={{0,4},{2,6},{4,0},{6,2},{1,5},{3,7},{5,1},{7,3},{8,12},{10,14},{12... | collective-permute-start | bytes 393224 | tf_op jit(solution)/shard_map/ppermute | solution.py:21
  6.0 3.1 %collective-permute-done.1.refs_1_ = bf16[512,128]{1,0:T(8,128)(2,1)S(1)} collective-permute-done((bf16[512,128]{1,0:T(8,128)(2,1)S(1)}, bf16[512,128]{1,0:T(8,128)(2,1)S(1)}, u32[]{:S(2)}, u32[]{:S(2)}) %collective-permute-start.1) | collective-permute-done | bytes 131104 | tf_op jit(solution)/shard_map/ppermute | solution.py:21
  9.1 2.0 %collective-permute-done.4.refs_0_ = bf16[512,128]{1,0:T(8,128)(2,1)S(1)} collective-permute-done((bf16[512,128]{1,0:T(8,128)(2,1)S(1)}, bf16[512,128]{1,0:T(8,128)(2,1)S(1)}, u32[]{:S(2)}, u32[]{:S(2)}) %collective-permute-start.4) | collective-permute-done | bytes 131104 | tf_op jit(solution)/shard_map/ppermute | solution.py:21
  11.1 7.1 %start.1 = (bf16[128,256,256]{2,1,0:T(8,128)(2,1)S(1)}, s32[4,256]{1,0:T(4,128)S(1)}, f32[16,256,128]{2,1,0:T(8,128)S(1)}) custom-call(s32[2,128]{1,0:T(2,128)S(1)} %pad_add_fusion.tables_hbm, bf16[128,256,256]{2,1,0:T(8,128)(2,1)} %bitcast.66, bf16[512,128]{1,0:T(8,128)(2,1)S(1)} %get-tuple-element.78.refs_0_, bf16[512,128]{1,0:T(8,128)(2,1)S(1)} %collective-permute-done.refs_1_), custom_call_target="tpu_custom_call" | custom-call | flops 2147483648 | tf_op jit(solution)/shard_map/start/pallas_call | solution.py:258
  18.2 4.3 %shard_map.68.before = f32[16,256,128]{2,1,0:T(8,128)S(1)} custom-call(s32[4,256]{1,0:T(4,128)S(1)} %get-tuple-element.29.plan_hbm, bf16[128,256,256]{2,1,0:T(8,128)(2,1)S(1)} %get-tuple-element.30.blocks_ref, f32[16,256,128]{2,1,0:T(8,128)S(1)} %get-tuple-element.31.refs_0_, bf16[512,128]{1,0:T(8,128)(2,1)S(1)} %collective-permute-done.1.refs_1_, ...), custom_call_target="tpu_custom_call" | custom-call | flops 1073741824 | tf_op jit(solution)/shard_map/pallas_call | solution.py:226
  22.5 2.0 %shard_map.70 = (bf16[1024,128]{1,0:T(8,128)(2,1)S(1)}, bf16[1024,128]{1,0:T(8,128)(2,1)S(1)}) custom-call(s32[4,256]{1,0:T(4,128)S(1)} %get-tuple-element.29.plan_hbm, bf16[128,256,256]{2,1,0:T(8,128)(2,1)S(1)} %get-tuple-element.30.blocks_ref, f32[16,256,128]{2,1,0:T(8,128)S(1)} %shard_map.68.before, bf16[512,128]{1,0:T(8,128)(2,1)S(1)} %collective-permute-done.4.refs_0_, ...), custom_call_target="tpu_custom_call" | custom-call | flops 257698032 | tf_op jit(solution)/shard_map/pallas_call | solution.py:237
  24.5 1.5 %collective-permute-start.6 = (bf16[1024,128]{1,0:T(8,128)(2,1)S(1)}, bf16[1024,128]{1,0:T(8,128)(2,1)S(1)}, u32[]{:S(2)}, u32[]{:S(2)}) collective-permute-start(bf16[1024,128]{1,0:T(8,128)(2,1)S(1)} %get-tuple-element.33), channel_id=1, source_target_pairs={{0,8},{8,0},{16,24},{24,16},{1,9},{9,1},{17,25},{25,17},{2,10},{10... | collective-permute-start | bytes 786440 | tf_op jit(solution)/shard_map/ppermute | solution.py:21
  26.6 2.0 %shard_map.69 = (f32[1024,128]{1,0:T(8,128)S(1)}, f32[1024,128]{1,0:T(8,128)S(1)}) custom-call(s32[4,256]{1,0:T(4,128)S(1)} %get-tuple-element.29.plan_hbm, bf16[128,256,256]{2,1,0:T(8,128)(2,1)S(1)} %get-tuple-element.30.blocks_ref, f32[16,256,128]{2,1,0:T(8,128)S(1)} %shard_map.68.before, bf16[512,128]{1,0:T(8,128)(2,1)S(1)} %collective-permute-done.4.refs_0_, ...), custom_call_target="tpu_custom_call" | custom-call | flops 257698032 | tf_op jit(solution)/shard_map/pallas_call | solution.py:237
  28.7 5.1 %collective-permute-done.6 = bf16[1024,128]{1,0:T(8,128)(2,1)S(1)} collective-permute-done((bf16[1024,128]{1,0:T(8,128)(2,1)S(1)}, bf16[1024,128]{1,0:T(8,128)(2,1)S(1)}, u32[]{:S(2)}, u32[]{:S(2)}) %collective-permute-start.6) | collective-permute-done | bytes 262176 | tf_op jit(solution)/shard_map/ppermute | solution.py:21
  33.8 2.3 %collective-permute-start.7 = (bf16[512,128]{1,0:T(8,128)(2,1)S(1)}, bf16[512,128]{1,0:T(8,128)(2,1)S(1)}, u32[]{:S(2)}, u32[]{:S(2)}) collective-permute-start(bf16[512,128]{1,0:T(8,128)(2,1)S(1)} %fusion.6), channel_id=1, source_target_pairs={{0,16},{8,24},{16,0},{24,8},{1,17},{9,25},{17,1},{25,9},{2,18},{10... | collective-permute-start | bytes 393224 | tf_op jit(solution)/shard_map/ppermute | solution.py:21
  36.1 5.2 %collective-permute-done.8 = bf16[1024,128]{1,0:T(8,128)(2,1)S(1)} collective-permute-done((bf16[1024,128]{1,0:T(8,128)(2,1)S(1)}, bf16[1024,128]{1,0:T(8,128)(2,1)S(1)}, u32[]{:S(2)}, u32[]{:S(2)}) %collective-permute-start.8) | collective-permute-done | bytes 262176 | tf_op jit(solution)/shard_map/ppermute | solution.py:21
  43.6 6.3 %collective-permute-done.9 = bf16[512,128]{1,0:T(8,128)(2,1)S(1)} collective-permute-done((bf16[512,128]{1,0:T(8,128)(2,1)S(1)}, bf16[512,128]{1,0:T(8,128)(2,1)S(1)}, u32[]{:S(2)}, u32[]{:S(2)}) %collective-permute-start.9) | collective-permute-done | bytes 131104 | tf_op jit(solution)/shard_map/ppermute | solution.py:21
  50.7 1.6 %collective-permute-start.14 = (bf16[512,128]{1,0:T(8,128)(2,1)S(1)}, bf16[512,128]{1,0:T(8,128)(2,1)S(1)}, u32[]{:S(2)}, u32[]{:S(2)}) collective-permute-start(bf16[512,128]{1,0:T(8,128)(2,1)S(1)} %get-tuple-element.72.refs_3_), channel_id=1, source_target_pairs={{0,4},{2,6},{4,0},{6,2},{1,5},{3,7},{5,1},{7,3},{8,12},{10,14},{12... | collective-permute-start | bytes 393224 | tf_op jit(solution)/shard_map/ppermute | solution.py:21
  52.3 2.1 %shard_map.71.refs_0_ = f32[16,256,128]{2,1,0:T(8,128)S(1)} custom-call(s32[4,256]{1,0:T(4,128)S(1)} %get-tuple-element.29.plan_hbm, bf16[128,256,256]{2,1,0:T(8,128)(2,1)S(1)} %get-tuple-element.30.blocks_ref, bf16[512,128]{1,0:T(8,128)(2,1)S(1)} %get-tuple-element.74.refs_0_, bf16[512,128]{1,0:T(8,128)(2,1)S(1)} %collective-permute-done.10.refs_1_), custom_call_target="tpu_custom_call" | custom-call | flops 536870912 | tf_op jit(solution)/shard_map/pallas_call | solution.py:226
  54.4 4.3 %shard_map.72.before = f32[16,256,128]{2,1,0:T(8,128)S(1)} custom-call(s32[4,256]{1,0:T(4,128)S(1)} %get-tuple-element.29.plan_hbm, bf16[128,256,256]{2,1,0:T(8,128)(2,1)S(1)} %get-tuple-element.30.blocks_ref, f32[16,256,128]{2,1,0:T(8,128)S(1)} %shard_map.71.refs_0_, bf16[512,128]{1,0:T(8,128)(2,1)S(1)} %collective-permute-done.11.refs_1_, ...), custom_call_target="tpu_custom_call" | custom-call | flops 1073741824 | tf_op jit(solution)/shard_map/pallas_call | solution.py:226
  60.2 2.0 %shard_map.74 = (bf16[1024,128]{1,0:T(8,128)(2,1)S(1)}, bf16[1024,128]{1,0:T(8,128)(2,1)S(1)}) custom-call(s32[4,256]{1,0:T(4,128)S(1)} %get-tuple-element.29.plan_hbm, bf16[128,256,256]{2,1,0:T(8,128)(2,1)S(1)} %get-tuple-element.30.blocks_ref, f32[16,256,128]{2,1,0:T(8,128)S(1)} %shard_map.72.before, bf16[512,128]{1,0:T(8,128)(2,1)S(1)} %collective-permute-done.14.refs_0_, ...), custom_call_target="tpu_custom_call" | custom-call | flops 257698032 | tf_op jit(solution)/shard_map/pallas_call | solution.py:237
  62.3 2.0 %collective-permute-start.18 = (bf16[1024,128]{1,0:T(8,128)(2,1)S(1)}, bf16[1024,128]{1,0:T(8,128)(2,1)S(1)}, u32[]{:S(2)}, u32[]{:S(2)}) collective-permute-start(bf16[1024,128]{1,0:T(8,128)(2,1)S(1)} %get-tuple-element.43), channel_id=1, source_target_pairs={{0,8},{8,0},{16,24},{24,16},{1,9},{9,1},{17,25},{25,17},{2,10},{10... | collective-permute-start | bytes 786440 | tf_op jit(solution)/shard_map/ppermute | solution.py:21
  64.3 2.0 %shard_map.73 = (f32[1024,128]{1,0:T(8,128)S(1)}, f32[1024,128]{1,0:T(8,128)S(1)}) custom-call(s32[4,256]{1,0:T(4,128)S(1)} %get-tuple-element.29.plan_hbm, bf16[128,256,256]{2,1,0:T(8,128)(2,1)S(1)} %get-tuple-element.30.blocks_ref, f32[16,256,128]{2,1,0:T(8,128)S(1)} %shard_map.72.before, bf16[512,128]{1,0:T(8,128)(2,1)S(1)} %collective-permute-done.14.refs_0_, ...), custom_call_target="tpu_custom_call" | custom-call | flops 257698032 | tf_op jit(solution)/shard_map/pallas_call | solution.py:237
  66.3 5.1 %collective-permute-done.16 = bf16[1024,128]{1,0:T(8,128)(2,1)S(1)} collective-permute-done((bf16[1024,128]{1,0:T(8,128)(2,1)S(1)}, bf16[1024,128]{1,0:T(8,128)(2,1)S(1)}, u32[]{:S(2)}, u32[]{:S(2)}) %collective-permute-start.16) | collective-permute-done | bytes 262176 | tf_op jit(solution)/shard_map/ppermute | solution.py:21
  71.6 5.7 %collective-permute-done.18 = bf16[1024,128]{1,0:T(8,128)(2,1)S(1)} collective-permute-done((bf16[1024,128]{1,0:T(8,128)(2,1)S(1)}, bf16[1024,128]{1,0:T(8,128)(2,1)S(1)}, u32[]{:S(2)}, u32[]{:S(2)}) %collective-permute-start.18) | collective-permute-done | bytes 262176 | tf_op jit(solution)/shard_map/ppermute | solution.py:21
  78.2 1.8 %collective-permute-done.17 = bf16[512,128]{1,0:T(8,128)(2,1)S(1)} collective-permute-done((bf16[512,128]{1,0:T(8,128)(2,1)S(1)}, bf16[512,128]{1,0:T(8,128)(2,1)S(1)}, u32[]{:S(2)}, u32[]{:S(2)}) %collective-permute-start.17) | collective-permute-done | bytes 131104 | tf_op jit(solution)/shard_map/ppermute | solution.py:21
  80.6 4.9 %collective-permute-done.19 = bf16[512,128]{1,0:T(8,128)(2,1)S(1)} collective-permute-done((bf16[512,128]{1,0:T(8,128)(2,1)S(1)}, bf16[512,128]{1,0:T(8,128)(2,1)S(1)}, u32[]{:S(2)}, u32[]{:S(2)}) %collective-permute-start.19) | collective-permute-done | bytes 131104 | tf_op jit(solution)/shard_map/ppermute | solution.py:21
  87.1 2.1 %shard_map.75.refs_0_ = f32[16,256,128]{2,1,0:T(8,128)S(1)} custom-call(s32[4,256]{1,0:T(4,128)S(1)} %get-tuple-element.29.plan_hbm, bf16[128,256,256]{2,1,0:T(8,128)(2,1)S(1)} %get-tuple-element.30.blocks_ref, bf16[512,128]{1,0:T(8,128)(2,1)S(1)} %convert_element_type.111.refs_0_, bf16[512,128]{1,0:T(8,128)(2,1)S(1)} %collective-permute-done.20.refs_1_), custom_call_target="tpu_custom_call" | custom-call | flops 536870912 | tf_op jit(solution)/shard_map/pallas_call | solution.py:226
  89.3 4.3 %shard_map.76.before = f32[16,256,128]{2,1,0:T(8,128)S(1)} custom-call(s32[4,256]{1,0:T(4,128)S(1)} %get-tuple-element.29.plan_hbm, bf16[128,256,256]{2,1,0:T(8,128)(2,1)S(1)} %get-tuple-element.30.blocks_ref, f32[16,256,128]{2,1,0:T(8,128)S(1)} %shard_map.75.refs_0_, bf16[512,128]{1,0:T(8,128)(2,1)S(1)} %collective-permute-done.21.refs_1_, ...), custom_call_target="tpu_custom_call" | custom-call | flops 1073741824 | tf_op jit(solution)/shard_map/pallas_call | solution.py:226
  95.0 2.0 %shard_map.78 = (bf16[1024,128]{1,0:T(8,128)(2,1)S(1)}, bf16[1024,128]{1,0:T(8,128)(2,1)S(1)}) custom-call(s32[4,256]{1,0:T(4,128)S(1)} %get-tuple-element.29.plan_hbm, bf16[128,256,256]{2,1,0:T(8,128)(2,1)S(1)} %get-tuple-element.30.blocks_ref, f32[16,256,128]{2,1,0:T(8,128)S(1)} %shard_map.76.before, bf16[512,128]{1,0:T(8,128)(2,1)S(1)} %collective-permute-done.24.refs_0_, ...), custom_call_target="tpu_custom_call" | custom-call | flops 257698032 | tf_op jit(solution)/shard_map/pallas_call | solution.py:237
  99.2 2.0 %shard_map.77 = (f32[1024,128]{1,0:T(8,128)S(1)}, f32[1024,128]{1,0:T(8,128)S(1)}) custom-call(s32[4,256]{1,0:T(4,128)S(1)} %get-tuple-element.29.plan_hbm, bf16[128,256,256]{2,1,0:T(8,128)(2,1)S(1)} %get-tuple-element.30.blocks_ref, f32[16,256,128]{2,1,0:T(8,128)S(1)} %shard_map.76.before, bf16[512,128]{1,0:T(8,128)(2,1)S(1)} %collective-permute-done.24.refs_0_, ...), custom_call_target="tpu_custom_call" | custom-call | flops 257698032 | tf_op jit(solution)/shard_map/pallas_call | solution.py:237
  101.3 9.5 %collective-permute-done.26 = bf16[1024,128]{1,0:T(8,128)(2,1)S(1)} collective-permute-done((bf16[1024,128]{1,0:T(8,128)(2,1)S(1)}, bf16[1024,128]{1,0:T(8,128)(2,1)S(1)}, u32[]{:S(2)}, u32[]{:S(2)}) %collective-permute-start.26) | collective-permute-done | bytes 262176 | tf_op jit(solution)/shard_map/ppermute | solution.py:21
  110.8 5.4 %collective-permute-done.27 = bf16[1024,128]{1,0:T(8,128)(2,1)S(1)} collective-permute-done((bf16[1024,128]{1,0:T(8,128)(2,1)S(1)}, bf16[1024,128]{1,0:T(8,128)(2,1)S(1)}, u32[]{:S(2)}, u32[]{:S(2)}) %collective-permute-start.27) | collective-permute-done | bytes 262176 | tf_op jit(solution)/shard_map/ppermute | solution.py:21
  120.3 1.8 %collective-permute-start.34 = (bf16[512,128]{1,0:T(8,128)(2,1)S(1)}, bf16[512,128]{1,0:T(8,128)(2,1)S(1)}, u32[]{:S(2)}, u32[]{:S(2)}) collective-permute-start(bf16[512,128]{1,0:T(8,128)(2,1)S(1)} %fusion.5), channel_id=1, source_target_pairs={{0,16},{8,24},{16,0},{24,8},{1,17},{9,25},{17,1},{25,9},{2,18},{10... | collective-permute-start | bytes 393224 | tf_op jit(solution)/shard_map/ppermute | solution.py:21
  122.9 3.1 %collective-permute-done.31 = f32[3,128]{1,0:T(4,128)S(1)} collective-permute-done((f32[3,128]{1,0:T(4,128)S(1)}, f32[3,128]{1,0:T(4,128)S(1)}, u32[]{:S(2)}, u32[]{:S(2)}) %collective-permute-start.31) | collective-permute-done | bytes 1568 | tf_op jit(solution)/shard_map/ppermute | solution.py:21
  126.0 3.0 %collective-permute-start.32 = (f32[3,128]{1,0:T(4,128)S(1)}, f32[3,128]{1,0:T(4,128)S(1)}, u32[]{:S(2)}, u32[]{:S(2)}) collective-permute-start(f32[3,128]{1,0:T(4,128)S(1)} %add.177), channel_id=1, source_target_pairs={{0,16},{8,24},{16,0},{24,8},{1,17},{9,25},{17,1},{25,9},{2,18},{10... | collective-permute-start | bytes 4616 | tf_op jit(solution)/shard_map/ppermute | solution.py:21
  129.0 4.9 %collective-permute-done.32 = f32[3,128]{1,0:T(4,128)S(1)} collective-permute-done((f32[3,128]{1,0:T(4,128)S(1)}, f32[3,128]{1,0:T(4,128)S(1)}, u32[]{:S(2)}, u32[]{:S(2)}) %collective-permute-start.32) | collective-permute-done | bytes 1568 | tf_op jit(solution)/shard_map/ppermute | solution.py:21
  (89 shorter events, 21.1 us)
Async XLA Ops:
  1.7 7.4 %collective-permute-start.1 = (bf16[512,128]{1,0:T(8,128)(2,1)S(1)}, bf16[512,128]{1,0:T(8,128)(2,1)S(1)}, u32[]{:S(2)}, u32[]{:S(2)}) collective-permute-start(bf16[512,128]{1,0:T(8,128)(2,1)S(1)} %get-tuple-element.78.refs_0_), channel_id=1, source_target_pairs={{0,4},{2,6},{4,0},{6,2},{1,5},{3,7},{5,1},{7,3},{8,12},{10,14},{12... | collective-permute-start | bytes 393224 | tf_op jit(solution)/shard_map/ppermute | solution.py:21
  4.8 6.3 %collective-permute-start.4 = (bf16[512,128]{1,0:T(8,128)(2,1)S(1)}, bf16[512,128]{1,0:T(8,128)(2,1)S(1)}, u32[]{:S(2)}, u32[]{:S(2)}) collective-permute-start(bf16[512,128]{1,0:T(8,128)(2,1)S(1)} %get-tuple-element.77.refs_3_), channel_id=1, source_target_pairs={{0,4},{2,6},{4,0},{6,2},{1,5},{3,7},{5,1},{7,3},{8,12},{10,14},{12... | collective-permute-start | bytes 393224 | tf_op jit(solution)/shard_map/ppermute | solution.py:21
  4.9 6.2 %collective-permute-start = (bf16[512,128]{1,0:T(8,128)(2,1)S(1)}, bf16[512,128]{1,0:T(8,128)(2,1)S(1)}, u32[]{:S(2)}, u32[]{:S(2)}) collective-permute-start(bf16[512,128]{1,0:T(8,128)(2,1)S(1)} %get-tuple-element.78.refs_0_), channel_id=1, source_target_pairs={{0,2},{2,0},{4,6},{6,4},{1,3},{3,1},{5,7},{7,5},{8,10},{10,8},{12,... | collective-permute-start | bytes 393224 | tf_op jit(solution)/shard_map/ppermute | solution.py:21
  4.9 13.3 %collective-permute-start.3 = (bf16[512,128]{1,0:T(8,128)(2,1)S(1)}, bf16[512,128]{1,0:T(8,128)(2,1)S(1)}, u32[]{:S(2)}, u32[]{:S(2)}) collective-permute-start(bf16[512,128]{1,0:T(8,128)(2,1)S(1)} %get-tuple-element.77.refs_3_), channel_id=1, source_target_pairs={{0,2},{2,0},{4,6},{6,4},{1,3},{3,1},{5,7},{7,5},{8,10},{10,8},{12,... | collective-permute-start | bytes 393224 | tf_op jit(solution)/shard_map/ppermute | solution.py:21
  9.1 9.1 %collective-permute-start.2 = (bf16[512,128]{1,0:T(8,128)(2,1)S(1)}, bf16[512,128]{1,0:T(8,128)(2,1)S(1)}, u32[]{:S(2)}, u32[]{:S(2)}) collective-permute-start(bf16[512,128]{1,0:T(8,128)(2,1)S(1)} %collective-permute-done.1.refs_1_), channel_id=1, source_target_pairs={{0,2},{2,0},{4,6},{6,4},{1,3},{3,1},{5,7},{7,5},{8,10},{10,8},{12,... | collective-permute-start | bytes 393224 | tf_op jit(solution)/shard_map/ppermute | solution.py:21
  11.1 11.4 %collective-permute-start.5 = (bf16[512,128]{1,0:T(8,128)(2,1)S(1)}, bf16[512,128]{1,0:T(8,128)(2,1)S(1)}, u32[]{:S(2)}, u32[]{:S(2)}) collective-permute-start(bf16[512,128]{1,0:T(8,128)(2,1)S(1)} %collective-permute-done.4.refs_0_), channel_id=1, source_target_pairs={{0,2},{2,0},{4,6},{6,4},{1,3},{3,1},{5,7},{7,5},{8,10},{10,8},{12,... | collective-permute-start | bytes 393224 | tf_op jit(solution)/shard_map/ppermute | solution.py:21
  24.5 9.2 %collective-permute-start.6 = (bf16[1024,128]{1,0:T(8,128)(2,1)S(1)}, bf16[1024,128]{1,0:T(8,128)(2,1)S(1)}, u32[]{:S(2)}, u32[]{:S(2)}) collective-permute-start(bf16[1024,128]{1,0:T(8,128)(2,1)S(1)} %get-tuple-element.33), channel_id=1, source_target_pairs={{0,8},{8,0},{16,24},{24,16},{1,9},{9,1},{17,25},{25,17},{2,10},{10... | collective-permute-start | bytes 786440 | tf_op jit(solution)/shard_map/ppermute | solution.py:21
  26.0 15.3 %collective-permute-start.8 = (bf16[1024,128]{1,0:T(8,128)(2,1)S(1)}, bf16[1024,128]{1,0:T(8,128)(2,1)S(1)}, u32[]{:S(2)}, u32[]{:S(2)}) collective-permute-start(bf16[1024,128]{1,0:T(8,128)(2,1)S(1)} %get-tuple-element.35), channel_id=1, source_target_pairs={{0,8},{8,0},{16,24},{24,16},{1,9},{9,1},{17,25},{25,17},{2,10},{10... | collective-permute-start | bytes 786440 | tf_op jit(solution)/shard_map/ppermute | solution.py:21
  33.8 8.6 %collective-permute-start.7 = (bf16[512,128]{1,0:T(8,128)(2,1)S(1)}, bf16[512,128]{1,0:T(8,128)(2,1)S(1)}, u32[]{:S(2)}, u32[]{:S(2)}) collective-permute-start(bf16[512,128]{1,0:T(8,128)(2,1)S(1)} %fusion.6), channel_id=1, source_target_pairs={{0,16},{8,24},{16,0},{24,8},{1,17},{9,25},{17,1},{25,9},{2,18},{10... | collective-permute-start | bytes 393224 | tf_op jit(solution)/shard_map/ppermute | solution.py:21
  41.5 8.5 %collective-permute-start.9 = (bf16[512,128]{1,0:T(8,128)(2,1)S(1)}, bf16[512,128]{1,0:T(8,128)(2,1)S(1)}, u32[]{:S(2)}, u32[]{:S(2)}) collective-permute-start(bf16[512,128]{1,0:T(8,128)(2,1)S(1)} %fusion.7), channel_id=1, source_target_pairs={{0,16},{8,24},{16,0},{24,8},{1,17},{9,25},{17,1},{25,9},{2,18},{10... | collective-permute-start | bytes 393224 | tf_op jit(solution)/shard_map/ppermute | solution.py:21
  42.6 9.8 %collective-permute-start.10 = (bf16[512,128]{1,0:T(8,128)(2,1)S(1)}, bf16[512,128]{1,0:T(8,128)(2,1)S(1)}, u32[]{:S(2)}, u32[]{:S(2)}) collective-permute-start(bf16[512,128]{1,0:T(8,128)(2,1)S(1)} %get-tuple-element.74.refs_0_), channel_id=1, source_target_pairs={{0,2},{2,0},{4,6},{6,4},{1,3},{3,1},{5,7},{7,5},{8,10},{10,8},{12,... | collective-permute-start | bytes 393224 | tf_op jit(solution)/shard_map/ppermute | solution.py:21
  42.6 7.6 %collective-permute-start.11 = (bf16[512,128]{1,0:T(8,128)(2,1)S(1)}, bf16[512,128]{1,0:T(8,128)(2,1)S(1)}, u32[]{:S(2)}, u32[]{:S(2)}) collective-permute-start(bf16[512,128]{1,0:T(8,128)(2,1)S(1)} %get-tuple-element.74.refs_0_), channel_id=1, source_target_pairs={{0,4},{2,6},{4,0},{6,2},{1,5},{3,7},{5,1},{7,3},{8,12},{10,14},{12... | collective-permute-start | bytes 393224 | tf_op jit(solution)/shard_map/ppermute | solution.py:21
  50.1 4.3 %collective-permute-start.13 = (bf16[512,128]{1,0:T(8,128)(2,1)S(1)}, bf16[512,128]{1,0:T(8,128)(2,1)S(1)}, u32[]{:S(2)}, u32[]{:S(2)}) collective-permute-start(bf16[512,128]{1,0:T(8,128)(2,1)S(1)} %get-tuple-element.72.refs_3_), channel_id=1, source_target_pairs={{0,2},{2,0},{4,6},{6,4},{1,3},{3,1},{5,7},{7,5},{8,10},{10,8},{12,... | collective-permute-start | bytes 393224 | tf_op jit(solution)/shard_map/ppermute | solution.py:21
  50.2 4.2 %collective-permute-start.12 = (bf16[512,128]{1,0:T(8,128)(2,1)S(1)}, bf16[512,128]{1,0:T(8,128)(2,1)S(1)}, u32[]{:S(2)}, u32[]{:S(2)}) collective-permute-start(bf16[512,128]{1,0:T(8,128)(2,1)S(1)} %collective-permute-done.11.refs_1_), channel_id=1, source_target_pairs={{0,2},{2,0},{4,6},{6,4},{1,3},{3,1},{5,7},{7,5},{8,10},{10,8},{12,... | collective-permute-start | bytes 393224 | tf_op jit(solution)/shard_map/ppermute | solution.py:21
  50.7 8.0 %collective-permute-start.14 = (bf16[512,128]{1,0:T(8,128)(2,1)S(1)}, bf16[512,128]{1,0:T(8,128)(2,1)S(1)}, u32[]{:S(2)}, u32[]{:S(2)}) collective-permute-start(bf16[512,128]{1,0:T(8,128)(2,1)S(1)} %get-tuple-element.72.refs_3_), channel_id=1, source_target_pairs={{0,4},{2,6},{4,0},{6,2},{1,5},{3,7},{5,1},{7,3},{8,12},{10,14},{12... | collective-permute-start | bytes 393224 | tf_op jit(solution)/shard_map/ppermute | solution.py:21
  62.2 9.2 %collective-permute-start.16 = (bf16[1024,128]{1,0:T(8,128)(2,1)S(1)}, bf16[1024,128]{1,0:T(8,128)(2,1)S(1)}, u32[]{:S(2)}, u32[]{:S(2)}) collective-permute-start(bf16[1024,128]{1,0:T(8,128)(2,1)S(1)} %get-tuple-element.41), channel_id=1, source_target_pairs={{0,8},{8,0},{16,24},{24,16},{1,9},{9,1},{17,25},{25,17},{2,10},{10... | collective-permute-start | bytes 786440 | tf_op jit(solution)/shard_map/ppermute | solution.py:21
  62.3 15.0 %collective-permute-start.18 = (bf16[1024,128]{1,0:T(8,128)(2,1)S(1)}, bf16[1024,128]{1,0:T(8,128)(2,1)S(1)}, u32[]{:S(2)}, u32[]{:S(2)}) collective-permute-start(bf16[1024,128]{1,0:T(8,128)(2,1)S(1)} %get-tuple-element.43), channel_id=1, source_target_pairs={{0,8},{8,0},{16,24},{24,16},{1,9},{9,1},{17,25},{25,17},{2,10},{10... | collective-permute-start | bytes 786440 | tf_op jit(solution)/shard_map/ppermute | solution.py:21
  71.5 8.5 %collective-permute-start.17 = (bf16[512,128]{1,0:T(8,128)(2,1)S(1)}, bf16[512,128]{1,0:T(8,128)(2,1)S(1)}, u32[]{:S(2)}, u32[]{:S(2)}) collective-permute-start(bf16[512,128]{1,0:T(8,128)(2,1)S(1)} %fusion.8), channel_id=1, source_target_pairs={{0,16},{8,24},{16,0},{24,8},{1,17},{9,25},{17,1},{25,9},{2,18},{10... | collective-permute-start | bytes 393224 | tf_op jit(solution)/shard_map/ppermute | solution.py:21
  77.3 8.1 %collective-permute-start.19 = (bf16[512,128]{1,0:T(8,128)(2,1)S(1)}, bf16[512,128]{1,0:T(8,128)(2,1)S(1)}, u32[]{:S(2)}, u32[]{:S(2)}) collective-permute-start(bf16[512,128]{1,0:T(8,128)(2,1)S(1)} %fusion.9), channel_id=1, source_target_pairs={{0,16},{8,24},{16,0},{24,8},{1,17},{9,25},{17,1},{25,9},{2,18},{10... | collective-permute-start | bytes 393224 | tf_op jit(solution)/shard_map/ppermute | solution.py:21
  80.3 6.9 %collective-permute-start.20 = (bf16[512,128]{1,0:T(8,128)(2,1)S(1)}, bf16[512,128]{1,0:T(8,128)(2,1)S(1)}, u32[]{:S(2)}, u32[]{:S(2)}) collective-permute-start(bf16[512,128]{1,0:T(8,128)(2,1)S(1)} %convert_element_type.111.refs_0_), channel_id=1, source_target_pairs={{0,2},{2,0},{4,6},{6,4},{1,3},{3,1},{5,7},{7,5},{8,10},{10,8},{12,... | collective-permute-start | bytes 393224 | tf_op jit(solution)/shard_map/ppermute | solution.py:21
  80.3 5.9 %collective-permute-start.21 = (bf16[512,128]{1,0:T(8,128)(2,1)S(1)}, bf16[512,128]{1,0:T(8,128)(2,1)S(1)}, u32[]{:S(2)}, u32[]{:S(2)}) collective-permute-start(bf16[512,128]{1,0:T(8,128)(2,1)S(1)} %convert_element_type.111.refs_0_), channel_id=1, source_target_pairs={{0,4},{2,6},{4,0},{6,2},{1,5},{3,7},{5,1},{7,3},{8,12},{10,14},{12... | collective-permute-start | bytes 393224 | tf_op jit(solution)/shard_map/ppermute | solution.py:21
  85.6 3.6 %collective-permute-start.23 = (bf16[512,128]{1,0:T(8,128)(2,1)S(1)}, bf16[512,128]{1,0:T(8,128)(2,1)S(1)}, u32[]{:S(2)}, u32[]{:S(2)}) collective-permute-start(bf16[512,128]{1,0:T(8,128)(2,1)S(1)} %get-tuple-element.70.refs_3_), channel_id=1, source_target_pairs={{0,2},{2,0},{4,6},{6,4},{1,3},{3,1},{5,7},{7,5},{8,10},{10,8},{12,... | collective-permute-start | bytes 393224 | tf_op jit(solution)/shard_map/ppermute | solution.py:21
  86.2 3.0 %collective-permute-start.22 = (bf16[512,128]{1,0:T(8,128)(2,1)S(1)}, bf16[512,128]{1,0:T(8,128)(2,1)S(1)}, u32[]{:S(2)}, u32[]{:S(2)}) collective-permute-start(bf16[512,128]{1,0:T(8,128)(2,1)S(1)} %collective-permute-done.21.refs_1_), channel_id=1, source_target_pairs={{0,2},{2,0},{4,6},{6,4},{1,3},{3,1},{5,7},{7,5},{8,10},{10,8},{12,... | collective-permute-start | bytes 393224 | tf_op jit(solution)/shard_map/ppermute | solution.py:21
  86.2 7.3 %collective-permute-start.24 = (bf16[512,128]{1,0:T(8,128)(2,1)S(1)}, bf16[512,128]{1,0:T(8,128)(2,1)S(1)}, u32[]{:S(2)}, u32[]{:S(2)}) collective-permute-start(bf16[512,128]{1,0:T(8,128)(2,1)S(1)} %get-tuple-element.70.refs_3_), channel_id=1, source_target_pairs={{0,4},{2,6},{4,0},{6,2},{1,5},{3,7},{5,1},{7,3},{8,12},{10,14},{12... | collective-permute-start | bytes 393224 | tf_op jit(solution)/shard_map/ppermute | solution.py:21
  97.0 13.8 %collective-permute-start.26 = (bf16[1024,128]{1,0:T(8,128)(2,1)S(1)}, bf16[1024,128]{1,0:T(8,128)(2,1)S(1)}, u32[]{:S(2)}, u32[]{:S(2)}) collective-permute-start(bf16[1024,128]{1,0:T(8,128)(2,1)S(1)} %get-tuple-element.49), channel_id=1, source_target_pairs={{0,8},{8,0},{16,24},{24,16},{1,9},{9,1},{17,25},{25,17},{2,10},{10... | collective-permute-start | bytes 786440 | tf_op jit(solution)/shard_map/ppermute | solution.py:21
  97.4 18.9 %collective-permute-start.28 = (bf16[1024,128]{1,0:T(8,128)(2,1)S(1)}, bf16[1024,128]{1,0:T(8,128)(2,1)S(1)}, u32[]{:S(2)}, u32[]{:S(2)}) collective-permute-start(bf16[1024,128]{1,0:T(8,128)(2,1)S(1)} %pad_maximum_fusion.1), channel_id=1, source_target_pairs={{0,16},{8,24},{16,0},{24,8},{1,17},{9,25},{17,1},{25,9},{2,18},{10... | collective-permute-start | bytes 786440 | tf_op jit(solution)/shard_map/ppermute | solution.py:21
  98.2 18.1 %collective-permute-start.27 = (bf16[1024,128]{1,0:T(8,128)(2,1)S(1)}, bf16[1024,128]{1,0:T(8,128)(2,1)S(1)}, u32[]{:S(2)}, u32[]{:S(2)}) collective-permute-start(bf16[1024,128]{1,0:T(8,128)(2,1)S(1)} %get-tuple-element.51), channel_id=1, source_target_pairs={{0,8},{8,0},{16,24},{24,16},{1,9},{9,1},{17,25},{25,17},{2,10},{10... | collective-permute-start | bytes 786440 | tf_op jit(solution)/shard_map/ppermute | solution.py:21
  117.8 4.3 %collective-permute-start.30 = (f32[3,128]{1,0:T(4,128)S(1)}, f32[3,128]{1,0:T(4,128)S(1)}, u32[]{:S(2)}, u32[]{:S(2)}) collective-permute-start(f32[3,128]{1,0:T(4,128)S(1)} %fusion.10), channel_id=1, source_target_pairs={{0,4},{2,6},{4,0},{6,2},{1,5},{3,7},{5,1},{7,3},{8,12},{10,14},{12... | collective-permute-start | bytes 4616 | tf_op jit(solution)/shard_map/ppermute | solution.py:21
  119.1 15.3 %collective-permute-start.33 = (bf16[512,128]{1,0:T(8,128)(2,1)S(1)}, bf16[512,128]{1,0:T(8,128)(2,1)S(1)}, u32[]{:S(2)}, u32[]{:S(2)}) collective-permute-start(bf16[512,128]{1,0:T(8,128)(2,1)S(1)} %fusion.4), channel_id=1, source_target_pairs={{0,16},{8,24},{16,0},{24,8},{1,17},{9,25},{17,1},{25,9},{2,18},{10... | collective-permute-start | bytes 393224 | tf_op jit(solution)/shard_map/ppermute | solution.py:21
  120.3 14.1 %collective-permute-start.34 = (bf16[512,128]{1,0:T(8,128)(2,1)S(1)}, bf16[512,128]{1,0:T(8,128)(2,1)S(1)}, u32[]{:S(2)}, u32[]{:S(2)}) collective-permute-start(bf16[512,128]{1,0:T(8,128)(2,1)S(1)} %fusion.5), channel_id=1, source_target_pairs={{0,16},{8,24},{16,0},{24,8},{1,17},{9,25},{17,1},{25,9},{2,18},{10... | collective-permute-start | bytes 393224 | tf_op jit(solution)/shard_map/ppermute | solution.py:21
  122.1 3.9 %collective-permute-start.31 = (f32[3,128]{1,0:T(4,128)S(1)}, f32[3,128]{1,0:T(4,128)S(1)}, u32[]{:S(2)}, u32[]{:S(2)}) collective-permute-start(f32[3,128]{1,0:T(4,128)S(1)} %fusion.16), channel_id=1, source_target_pairs={{0,8},{8,0},{16,24},{24,16},{1,9},{9,1},{17,25},{25,17},{2,10},{10... | collective-permute-start | bytes 4616 | tf_op jit(solution)/shard_map/ppermute | solution.py:21
  126.0 7.9 %collective-permute-start.32 = (f32[3,128]{1,0:T(4,128)S(1)}, f32[3,128]{1,0:T(4,128)S(1)}, u32[]{:S(2)}, u32[]{:S(2)}) collective-permute-start(f32[3,128]{1,0:T(4,128)S(1)} %add.177), channel_id=1, source_target_pairs={{0,16},{8,24},{16,0},{24,8},{1,17},{9,25},{17,1},{25,9},{2,18},{10... | collective-permute-start | bytes 4616 | tf_op jit(solution)/shard_map/ppermute | solution.py:21
  (5 other events, 21.4 us)

commit v4 on v3

--- a/solution.py
+++ b/solution.py
@@ -313,19 +313,23 @@
         form3 += 2.0 * (dot(signs, [v[0] for v in last]) + dot(far_signs, [v[1] for v in last]))
         total = jnp.stack([dot(signs, first), dot(signs, second), form3])
         mask, sums = 1, [total]
-        while mask < n_gy:
+        while mask < lay.top:
             total = total + swap(total, "gy", mask)
-            sums.append(total)
             mask *= 2
-        mask = 1
+        total = total + swap(total, "gy", lay.top) + swap(total, "gx", 1) + swap(total, ("gx", "gy"), n_gy + lay.top)
+        sums.append(total)
+        mask = 2
         while mask < n_gx:
-            total = total + swap(total, "gx", mask)
+            got = swap(total, "gx", mask)
             mask *= 2
-        forms.append(total)
+            if mask < n_gx:
+                total = total + got
+        forms.extend((total, got))
         return sums[0], sums[-1]
 
     third = apply_operator(2, second, first, 2.0, add_forms)
-    return (forms[0], jnp.concatenate(third))
+    third = jnp.concatenate(third)
+    return (forms[0] + after(forms[1], third), third)
 
 
 def solution(mesh):

time: 136 us -> 137 us (level)
  waiting for transfers between devices: 66.3 us -> 68.6 us
    ppermute x35 -> x36, waiting for transfers between devices: 66.3 us -> 68.6 us  [swap(): return lax.ppermute(value, axis, [(d, d ^ mask) for d in range(n)])]
    ppermute x35 -> x36, starting transfers between devices: 27.1 us -> 26.4 us  [swap(): return lax.ppermute(value, axis, [(d, d ^ mask) for d in range(n)])]
  transfers between devices with their start and end apart: 35 -> 36, of which waited for: 17 -> 16; matrix products, arithmetic and copies ran while one was open for 2% -> 2% of each run, Pallas kernels for 22% -> 22%
where the time goes in v4:
time: 137 us
  waiting for transfers between devices  68.6 us (50%)
  Pallas kernels  36.2 us (26%)
  starting transfers between devices  26.4 us (19%)
  other arithmetic  4.85 us (4%)
    ppermute x36, waiting for transfers between devices, swap(): return lax.ppermute(value, axis, [(d, d ^ mask) for d in range(n)])  68.6 us
    ppermute x36, starting transfers between devices, swap(): return lax.ppermute(value, axis, [(d, d ^ mask) for d in range(n)])  26.4 us
    pallas_call x5, Pallas kernels, early(): pl.pallas_call(functools.partial(early_kernel, lay, number), out_shape=ja...  17 us
    pallas_call x6, Pallas kernels, late(): pl.pallas_call(functools.partial(late_kernel, lay, number), out_shape=tup...  12.1 us
    pallas_call x1, Pallas kernels, multiply(): held, plan, total = begin(tables, blocks[0, 0], *sum(near[:-1], []))  7.06 us
  transfers between devices with their start and end apart: 36, of which 16 were waited for; matrix products, arithmetic and copies ran while one was open for 2% of the time, Pallas kernels for 22%

profile of v4, /device:TPU:0, one launch (start us, length us, event | category | flops | bytes accessed | tf_op | source)
XLA Modules:
  0.0 137.3 jit_solution(14149397401390354221)
XLA Ops:
  1.7 3.0 %collective-permute-start.1 = (bf16[512,128]{1,0:T(8,128)(2,1)S(1)}, bf16[512,128]{1,0:T(8,128)(2,1)S(1)}, u32[]{:S(2)}, u32[]{:S(2)}) collective-permute-start(bf16[512,128]{1,0:T(8,128)(2,1)S(1)} %get-tuple-element.80.refs_0_), channel_id=1, source_target_pairs={{0,4},{2,6},{4,0},{6,2},{1,5},{3,7},{5,1},{7,3},{8,12},{10,14},{12... | collective-permute-start | bytes 393224 | tf_op jit(solution)/shard_map/ppermute | solution.py:21
  6.0 3.1 %collective-permute-done.1.refs_1_ = bf16[512,128]{1,0:T(8,128)(2,1)S(1)} collective-permute-done((bf16[512,128]{1,0:T(8,128)(2,1)S(1)}, bf16[512,128]{1,0:T(8,128)(2,1)S(1)}, u32[]{:S(2)}, u32[]{:S(2)}) %collective-permute-start.1) | collective-permute-done | bytes 131104 | tf_op jit(solution)/shard_map/ppermute | solution.py:21
  9.1 2.0 %collective-permute-done.4.refs_0_ = bf16[512,128]{1,0:T(8,128)(2,1)S(1)} collective-permute-done((bf16[512,128]{1,0:T(8,128)(2,1)S(1)}, bf16[512,128]{1,0:T(8,128)(2,1)S(1)}, u32[]{:S(2)}, u32[]{:S(2)}) %collective-permute-start.4) | collective-permute-done | bytes 131104 | tf_op jit(solution)/shard_map/ppermute | solution.py:21
  11.1 7.1 %start.1 = (bf16[128,256,256]{2,1,0:T(8,128)(2,1)S(1)}, s32[4,256]{1,0:T(4,128)S(1)}, f32[16,256,128]{2,1,0:T(8,128)S(1)}) custom-call(s32[2,128]{1,0:T(2,128)S(1)} %pad_add_fusion.tables_hbm, bf16[128,256,256]{2,1,0:T(8,128)(2,1)} %bitcast.66, bf16[512,128]{1,0:T(8,128)(2,1)S(1)} %get-tuple-element.80.refs_0_, bf16[512,128]{1,0:T(8,128)(2,1)S(1)} %collective-permute-done.refs_1_), custom_call_target="tpu_custom_call" | custom-call | flops 2147483648 | tf_op jit(solution)/shard_map/start/pallas_call | solution.py:258
  18.2 4.3 %shard_map.68.before = f32[16,256,128]{2,1,0:T(8,128)S(1)} custom-call(s32[4,256]{1,0:T(4,128)S(1)} %get-tuple-element.30.plan_hbm, bf16[128,256,256]{2,1,0:T(8,128)(2,1)S(1)} %get-tuple-element.31.blocks_ref, f32[16,256,128]{2,1,0:T(8,128)S(1)} %get-tuple-element.32.refs_0_, bf16[512,128]{1,0:T(8,128)(2,1)S(1)} %collective-permute-done.1.refs_1_, ...), custom_call_target="tpu_custom_call" | custom-call | flops 1073741824 | tf_op jit(solution)/shard_map/pallas_call | solution.py:226
  22.5 2.0 %shard_map.70 = (bf16[1024,128]{1,0:T(8,128)(2,1)S(1)}, bf16[1024,128]{1,0:T(8,128)(2,1)S(1)}) custom-call(s32[4,256]{1,0:T(4,128)S(1)} %get-tuple-element.30.plan_hbm, bf16[128,256,256]{2,1,0:T(8,128)(2,1)S(1)} %get-tuple-element.31.blocks_ref, f32[16,256,128]{2,1,0:T(8,128)S(1)} %shard_map.68.before, bf16[512,128]{1,0:T(8,128)(2,1)S(1)} %collective-permute-done.4.refs_0_, ...), custom_call_target="tpu_custom_call" | custom-call | flops 257698032 | tf_op jit(solution)/shard_map/pallas_call | solution.py:237
  24.5 1.5 %collective-permute-start.6 = (bf16[1024,128]{1,0:T(8,128)(2,1)S(1)}, bf16[1024,128]{1,0:T(8,128)(2,1)S(1)}, u32[]{:S(2)}, u32[]{:S(2)}) collective-permute-start(bf16[1024,128]{1,0:T(8,128)(2,1)S(1)} %get-tuple-element.34), channel_id=1, source_target_pairs={{0,8},{8,0},{16,24},{24,16},{1,9},{9,1},{17,25},{25,17},{2,10},{10... | collective-permute-start | bytes 786440 | tf_op jit(solution)/shard_map/ppermute | solution.py:21
  26.6 2.0 %shard_map.69 = (f32[1024,128]{1,0:T(8,128)S(1)}, f32[1024,128]{1,0:T(8,128)S(1)}) custom-call(s32[4,256]{1,0:T(4,128)S(1)} %get-tuple-element.30.plan_hbm, bf16[128,256,256]{2,1,0:T(8,128)(2,1)S(1)} %get-tuple-element.31.blocks_ref, f32[16,256,128]{2,1,0:T(8,128)S(1)} %shard_map.68.before, bf16[512,128]{1,0:T(8,128)(2,1)S(1)} %collective-permute-done.4.refs_0_, ...), custom_call_target="tpu_custom_call" | custom-call | flops 257698032 | tf_op jit(solution)/shard_map/pallas_call | solution.py:237
  28.7 5.1 %collective-permute-done.6 = bf16[1024,128]{1,0:T(8,128)(2,1)S(1)} collective-permute-done((bf16[1024,128]{1,0:T(8,128)(2,1)S(1)}, bf16[1024,128]{1,0:T(8,128)(2,1)S(1)}, u32[]{:S(2)}, u32[]{:S(2)}) %collective-permute-start.6) | collective-permute-done | bytes 262176 | tf_op jit(solution)/shard_map/ppermute | solution.py:21
  33.8 2.3 %collective-permute-start.7 = (bf16[512,128]{1,0:T(8,128)(2,1)S(1)}, bf16[512,128]{1,0:T(8,128)(2,1)S(1)}, u32[]{:S(2)}, u32[]{:S(2)}) collective-permute-start(bf16[512,128]{1,0:T(8,128)(2,1)S(1)} %fusion.6), channel_id=1, source_target_pairs={{0,16},{8,24},{16,0},{24,8},{1,17},{9,25},{17,1},{25,9},{2,18},{10... | collective-permute-start | bytes 393224 | tf_op jit(solution)/shard_map/ppermute | solution.py:21
  36.1 5.2 %collective-permute-done.8 = bf16[1024,128]{1,0:T(8,128)(2,1)S(1)} collective-permute-done((bf16[1024,128]{1,0:T(8,128)(2,1)S(1)}, bf16[1024,128]{1,0:T(8,128)(2,1)S(1)}, u32[]{:S(2)}, u32[]{:S(2)}) %collective-permute-start.8) | collective-permute-done | bytes 262176 | tf_op jit(solution)/shard_map/ppermute | solution.py:21
  43.6 6.3 %collective-permute-done.9 = bf16[512,128]{1,0:T(8,128)(2,1)S(1)} collective-permute-done((bf16[512,128]{1,0:T(8,128)(2,1)S(1)}, bf16[512,128]{1,0:T(8,128)(2,1)S(1)}, u32[]{:S(2)}, u32[]{:S(2)}) %collective-permute-start.9) | collective-permute-done | bytes 131104 | tf_op jit(solution)/shard_map/ppermute | solution.py:21
  50.7 1.6 %collective-permute-start.14 = (bf16[512,128]{1,0:T(8,128)(2,1)S(1)}, bf16[512,128]{1,0:T(8,128)(2,1)S(1)}, u32[]{:S(2)}, u32[]{:S(2)}) collective-permute-start(bf16[512,128]{1,0:T(8,128)(2,1)S(1)} %get-tuple-element.74.refs_3_), channel_id=1, source_target_pairs={{0,4},{2,6},{4,0},{6,2},{1,5},{3,7},{5,1},{7,3},{8,12},{10,14},{12... | collective-permute-start | bytes 393224 | tf_op jit(solution)/shard_map/ppermute | solution.py:21
  52.3 2.1 %shard_map.71.refs_0_ = f32[16,256,128]{2,1,0:T(8,128)S(1)} custom-call(s32[4,256]{1,0:T(4,128)S(1)} %get-tuple-element.30.plan_hbm, bf16[128,256,256]{2,1,0:T(8,128)(2,1)S(1)} %get-tuple-element.31.blocks_ref, bf16[512,128]{1,0:T(8,128)(2,1)S(1)} %get-tuple-element.76.refs_0_, bf16[512,128]{1,0:T(8,128)(2,1)S(1)} %collective-permute-done.10.refs_1_), custom_call_target="tpu_custom_call" | custom-call | flops 536870912 | tf_op jit(solution)/shard_map/pallas_call | solution.py:226
  54.4 4.3 %shard_map.72.before = f32[16,256,128]{2,1,0:T(8,128)S(1)} custom-call(s32[4,256]{1,0:T(4,128)S(1)} %get-tuple-element.30.plan_hbm, bf16[128,256,256]{2,1,0:T(8,128)(2,1)S(1)} %get-tuple-element.31.blocks_ref, f32[16,256,128]{2,1,0:T(8,128)S(1)} %shard_map.71.refs_0_, bf16[512,128]{1,0:T(8,128)(2,1)S(1)} %collective-permute-done.11.refs_1_, ...), custom_call_target="tpu_custom_call" | custom-call | flops 1073741824 | tf_op jit(solution)/shard_map/pallas_call | solution.py:226
  58.8 1.3 collective-permute-done.15.refs_1_
  60.2 2.0 %shard_map.74 = (bf16[1024,128]{1,0:T(8,128)(2,1)S(1)}, bf16[1024,128]{1,0:T(8,128)(2,1)S(1)}) custom-call(s32[4,256]{1,0:T(4,128)S(1)} %get-tuple-element.30.plan_hbm, bf16[128,256,256]{2,1,0:T(8,128)(2,1)S(1)} %get-tuple-element.31.blocks_ref, f32[16,256,128]{2,1,0:T(8,128)S(1)} %shard_map.72.before, bf16[512,128]{1,0:T(8,128)(2,1)S(1)} %collective-permute-done.14.refs_0_, ...), custom_call_target="tpu_custom_call" | custom-call | flops 257698032 | tf_op jit(solution)/shard_map/pallas_call | solution.py:237
  62.3 2.0 %collective-permute-start.18 = (bf16[1024,128]{1,0:T(8,128)(2,1)S(1)}, bf16[1024,128]{1,0:T(8,128)(2,1)S(1)}, u32[]{:S(2)}, u32[]{:S(2)}) collective-permute-start(bf16[1024,128]{1,0:T(8,128)(2,1)S(1)} %get-tuple-element.44), channel_id=1, source_target_pairs={{0,8},{8,0},{16,24},{24,16},{1,9},{9,1},{17,25},{25,17},{2,10},{10... | collective-permute-start | bytes 786440 | tf_op jit(solution)/shard_map/ppermute | solution.py:21
  64.3 2.0 %shard_map.73 = (f32[1024,128]{1,0:T(8,128)S(1)}, f32[1024,128]{1,0:T(8,128)S(1)}) custom-call(s32[4,256]{1,0:T(4,128)S(1)} %get-tuple-element.30.plan_hbm, bf16[128,256,256]{2,1,0:T(8,128)(2,1)S(1)} %get-tuple-element.31.blocks_ref, f32[16,256,128]{2,1,0:T(8,128)S(1)} %shard_map.72.before, bf16[512,128]{1,0:T(8,128)(2,1)S(1)} %collective-permute-done.14.refs_0_, ...), custom_call_target="tpu_custom_call" | custom-call | flops 257698032 | tf_op jit(solution)/shard_map/pallas_call | solution.py:237
  66.3 5.1 %collective-permute-done.16 = bf16[1024,128]{1,0:T(8,128)(2,1)S(1)} collective-permute-done((bf16[1024,128]{1,0:T(8,128)(2,1)S(1)}, bf16[1024,128]{1,0:T(8,128)(2,1)S(1)}, u32[]{:S(2)}, u32[]{:S(2)}) %collective-permute-start.16) | collective-permute-done | bytes 262176 | tf_op jit(solution)/shard_map/ppermute | solution.py:21
  71.6 5.7 %collective-permute-done.18 = bf16[1024,128]{1,0:T(8,128)(2,1)S(1)} collective-permute-done((bf16[1024,128]{1,0:T(8,128)(2,1)S(1)}, bf16[1024,128]{1,0:T(8,128)(2,1)S(1)}, u32[]{:S(2)}, u32[]{:S(2)}) %collective-permute-start.18) | collective-permute-done | bytes 262176 | tf_op jit(solution)/shard_map/ppermute | solution.py:21
  78.2 1.8 %collective-permute-done.17 = bf16[512,128]{1,0:T(8,128)(2,1)S(1)} collective-permute-done((bf16[512,128]{1,0:T(8,128)(2,1)S(1)}, bf16[512,128]{1,0:T(8,128)(2,1)S(1)}, u32[]{:S(2)}, u32[]{:S(2)}) %collective-permute-start.17) | collective-permute-done | bytes 131104 | tf_op jit(solution)/shard_map/ppermute | solution.py:21
  80.6 4.9 %collective-permute-done.19 = bf16[512,128]{1,0:T(8,128)(2,1)S(1)} collective-permute-done((bf16[512,128]{1,0:T(8,128)(2,1)S(1)}, bf16[512,128]{1,0:T(8,128)(2,1)S(1)}, u32[]{:S(2)}, u32[]{:S(2)}) %collective-permute-start.19) | collective-permute-done | bytes 131104 | tf_op jit(solution)/shard_map/ppermute | solution.py:21
  87.1 2.1 %shard_map.75.refs_0_ = f32[16,256,128]{2,1,0:T(8,128)S(1)} custom-call(s32[4,256]{1,0:T(4,128)S(1)} %get-tuple-element.30.plan_hbm, bf16[128,256,256]{2,1,0:T(8,128)(2,1)S(1)} %get-tuple-element.31.blocks_ref, bf16[512,128]{1,0:T(8,128)(2,1)S(1)} %convert_element_type.111.refs_0_, bf16[512,128]{1,0:T(8,128)(2,1)S(1)} %collective-permute-done.20.refs_1_), custom_call_target="tpu_custom_call" | custom-call | flops 536870912 | tf_op jit(solution)/shard_map/pallas_call | solution.py:226
  89.3 4.3 %shard_map.76.before = f32[16,256,128]{2,1,0:T(8,128)S(1)} custom-call(s32[4,256]{1,0:T(4,128)S(1)} %get-tuple-element.30.plan_hbm, bf16[128,256,256]{2,1,0:T(8,128)(2,1)S(1)} %get-tuple-element.31.blocks_ref, f32[16,256,128]{2,1,0:T(8,128)S(1)} %shard_map.75.refs_0_, bf16[512,128]{1,0:T(8,128)(2,1)S(1)} %collective-permute-done.21.refs_1_, ...), custom_call_target="tpu_custom_call" | custom-call | flops 1073741824 | tf_op jit(solution)/shard_map/pallas_call | solution.py:226
  95.0 2.0 %shard_map.78 = (bf16[1024,128]{1,0:T(8,128)(2,1)S(1)}, bf16[1024,128]{1,0:T(8,128)(2,1)S(1)}) custom-call(s32[4,256]{1,0:T(4,128)S(1)} %get-tuple-element.30.plan_hbm, bf16[128,256,256]{2,1,0:T(8,128)(2,1)S(1)} %get-tuple-element.31.blocks_ref, f32[16,256,128]{2,1,0:T(8,128)S(1)} %shard_map.76.before, bf16[512,128]{1,0:T(8,128)(2,1)S(1)} %collective-permute-done.24.refs_0_, ...), custom_call_target="tpu_custom_call" | custom-call | flops 257698032 | tf_op jit(solution)/shard_map/pallas_call | solution.py:237
  99.2 2.0 %shard_map.77 = (f32[1024,128]{1,0:T(8,128)S(1)}, f32[1024,128]{1,0:T(8,128)S(1)}) custom-call(s32[4,256]{1,0:T(4,128)S(1)} %get-tuple-element.30.plan_hbm, bf16[128,256,256]{2,1,0:T(8,128)(2,1)S(1)} %get-tuple-element.31.blocks_ref, f32[16,256,128]{2,1,0:T(8,128)S(1)} %shard_map.76.before, bf16[512,128]{1,0:T(8,128)(2,1)S(1)} %collective-permute-done.24.refs_0_, ...), custom_call_target="tpu_custom_call" | custom-call | flops 257698032 | tf_op jit(solution)/shard_map/pallas_call | solution.py:237
  101.3 9.5 %collective-permute-done.26 = bf16[1024,128]{1,0:T(8,128)(2,1)S(1)} collective-permute-done((bf16[1024,128]{1,0:T(8,128)(2,1)S(1)}, bf16[1024,128]{1,0:T(8,128)(2,1)S(1)}, u32[]{:S(2)}, u32[]{:S(2)}) %collective-permute-start.26) | collective-permute-done | bytes 262176 | tf_op jit(solution)/shard_map/ppermute | solution.py:21
  110.8 5.4 %collective-permute-done.27 = bf16[1024,128]{1,0:T(8,128)(2,1)S(1)} collective-permute-done((bf16[1024,128]{1,0:T(8,128)(2,1)S(1)}, bf16[1024,128]{1,0:T(8,128)(2,1)S(1)}, u32[]{:S(2)}, u32[]{:S(2)}) %collective-permute-start.27) | collective-permute-done | bytes 262176 | tf_op jit(solution)/shard_map/ppermute | solution.py:21
  117.8 1.5 %collective-permute-start.32 = (f32[3,128]{1,0:T(4,128)S(1)}, f32[3,128]{1,0:T(4,128)S(1)}, u32[]{:S(2)}, u32[]{:S(2)}) collective-permute-start(f32[3,128]{1,0:T(4,128)S(1)} %fusion.10), channel_id=1, source_target_pairs={{0,12},{2,14},{4,8},{6,10},{8,4},{10,6},{12,0},{14,2},{16,28},{18,... | collective-permute-start | bytes 4616 | tf_op jit(solution)/shard_map/ppermute | solution.py:21
  122.1 2.3 %collective-permute-start.35 = (bf16[512,128]{1,0:T(8,128)(2,1)S(1)}, bf16[512,128]{1,0:T(8,128)(2,1)S(1)}, u32[]{:S(2)}, u32[]{:S(2)}) collective-permute-start(bf16[512,128]{1,0:T(8,128)(2,1)S(1)} %fusion.5), channel_id=1, source_target_pairs={{0,16},{8,24},{16,0},{24,8},{1,17},{9,25},{17,1},{25,9},{2,18},{10... | collective-permute-start | bytes 393224 | tf_op jit(solution)/shard_map/ppermute | solution.py:21
  125.4 10.2 %collective-permute-done.35 = bf16[512,128]{1,0:T(8,128)(2,1)S(1)} collective-permute-done((bf16[512,128]{1,0:T(8,128)(2,1)S(1)}, bf16[512,128]{1,0:T(8,128)(2,1)S(1)}, u32[]{:S(2)}, u32[]{:S(2)}) %collective-permute-start.35) | collective-permute-done | bytes 131104 | tf_op jit(solution)/shard_map/ppermute | solution.py:21
  (90 shorter events, 20.2 us)
Async XLA Ops:
  1.7 7.4 %collective-permute-start.1 = (bf16[512,128]{1,0:T(8,128)(2,1)S(1)}, bf16[512,128]{1,0:T(8,128)(2,1)S(1)}, u32[]{:S(2)}, u32[]{:S(2)}) collective-permute-start(bf16[512,128]{1,0:T(8,128)(2,1)S(1)} %get-tuple-element.80.refs_0_), channel_id=1, source_target_pairs={{0,4},{2,6},{4,0},{6,2},{1,5},{3,7},{5,1},{7,3},{8,12},{10,14},{12... | collective-permute-start | bytes 393224 | tf_op jit(solution)/shard_map/ppermute | solution.py:21
  4.8 6.3 %collective-permute-start.4 = (bf16[512,128]{1,0:T(8,128)(2,1)S(1)}, bf16[512,128]{1,0:T(8,128)(2,1)S(1)}, u32[]{:S(2)}, u32[]{:S(2)}) collective-permute-start(bf16[512,128]{1,0:T(8,128)(2,1)S(1)} %get-tuple-element.79.refs_3_), channel_id=1, source_target_pairs={{0,4},{2,6},{4,0},{6,2},{1,5},{3,7},{5,1},{7,3},{8,12},{10,14},{12... | collective-permute-start | bytes 393224 | tf_op jit(solution)/shard_map/ppermute | solution.py:21
  4.9 6.2 %collective-permute-start = (bf16[512,128]{1,0:T(8,128)(2,1)S(1)}, bf16[512,128]{1,0:T(8,128)(2,1)S(1)}, u32[]{:S(2)}, u32[]{:S(2)}) collective-permute-start(bf16[512,128]{1,0:T(8,128)(2,1)S(1)} %get-tuple-element.80.refs_0_), channel_id=1, source_target_pairs={{0,2},{2,0},{4,6},{6,4},{1,3},{3,1},{5,7},{7,5},{8,10},{10,8},{12,... | collective-permute-start | bytes 393224 | tf_op jit(solution)/shard_map/ppermute | solution.py:21
  4.9 13.3 %collective-permute-start.3 = (bf16[512,128]{1,0:T(8,128)(2,1)S(1)}, bf16[512,128]{1,0:T(8,128)(2,1)S(1)}, u32[]{:S(2)}, u32[]{:S(2)}) collective-permute-start(bf16[512,128]{1,0:T(8,128)(2,1)S(1)} %get-tuple-element.79.refs_3_), channel_id=1, source_target_pairs={{0,2},{2,0},{4,6},{6,4},{1,3},{3,1},{5,7},{7,5},{8,10},{10,8},{12,... | collective-permute-start | bytes 393224 | tf_op jit(solution)/shard_map/ppermute | solution.py:21
  9.1 9.1 %collective-permute-start.2 = (bf16[512,128]{1,0:T(8,128)(2,1)S(1)}, bf16[512,128]{1,0:T(8,128)(2,1)S(1)}, u32[]{:S(2)}, u32[]{:S(2)}) collective-permute-start(bf16[512,128]{1,0:T(8,128)(2,1)S(1)} %collective-permute-done.1.refs_1_), channel_id=1, source_target_pairs={{0,2},{2,0},{4,6},{6,4},{1,3},{3,1},{5,7},{7,5},{8,10},{10,8},{12,... | collective-permute-start | bytes 393224 | tf_op jit(solution)/shard_map/ppermute | solution.py:21
  11.1 11.4 %collective-permute-start.5 = (bf16[512,128]{1,0:T(8,128)(2,1)S(1)}, bf16[512,128]{1,0:T(8,128)(2,1)S(1)}, u32[]{:S(2)}, u32[]{:S(2)}) collective-permute-start(bf16[512,128]{1,0:T(8,128)(2,1)S(1)} %collective-permute-done.4.refs_0_), channel_id=1, source_target_pairs={{0,2},{2,0},{4,6},{6,4},{1,3},{3,1},{5,7},{7,5},{8,10},{10,8},{12,... | collective-permute-start | bytes 393224 | tf_op jit(solution)/shard_map/ppermute | solution.py:21
  24.5 9.2 %collective-permute-start.6 = (bf16[1024,128]{1,0:T(8,128)(2,1)S(1)}, bf16[1024,128]{1,0:T(8,128)(2,1)S(1)}, u32[]{:S(2)}, u32[]{:S(2)}) collective-permute-start(bf16[1024,128]{1,0:T(8,128)(2,1)S(1)} %get-tuple-element.34), channel_id=1, source_target_pairs={{0,8},{8,0},{16,24},{24,16},{1,9},{9,1},{17,25},{25,17},{2,10},{10... | collective-permute-start | bytes 786440 | tf_op jit(solution)/shard_map/ppermute | solution.py:21
  26.0 15.3 %collective-permute-start.8 = (bf16[1024,128]{1,0:T(8,128)(2,1)S(1)}, bf16[1024,128]{1,0:T(8,128)(2,1)S(1)}, u32[]{:S(2)}, u32[]{:S(2)}) collective-permute-start(bf16[1024,128]{1,0:T(8,128)(2,1)S(1)} %get-tuple-element.36), channel_id=1, source_target_pairs={{0,8},{8,0},{16,24},{24,16},{1,9},{9,1},{17,25},{25,17},{2,10},{10... | collective-permute-start | bytes 786440 | tf_op jit(solution)/shard_map/ppermute | solution.py:21
  33.8 8.6 %collective-permute-start.7 = (bf16[512,128]{1,0:T(8,128)(2,1)S(1)}, bf16[512,128]{1,0:T(8,128)(2,1)S(1)}, u32[]{:S(2)}, u32[]{:S(2)}) collective-permute-start(bf16[512,128]{1,0:T(8,128)(2,1)S(1)} %fusion.6), channel_id=1, source_target_pairs={{0,16},{8,24},{16,0},{24,8},{1,17},{9,25},{17,1},{25,9},{2,18},{10... | collective-permute-start | bytes 393224 | tf_op jit(solution)/shard_map/ppermute | solution.py:21
  41.5 8.5 %collective-permute-start.9 = (bf16[512,128]{1,0:T(8,128)(2,1)S(1)}, bf16[512,128]{1,0:T(8,128)(2,1)S(1)}, u32[]{:S(2)}, u32[]{:S(2)}) collective-permute-start(bf16[512,128]{1,0:T(8,128)(2,1)S(1)} %fusion.7), channel_id=1, source_target_pairs={{0,16},{8,24},{16,0},{24,8},{1,17},{9,25},{17,1},{25,9},{2,18},{10... | collective-permute-start | bytes 393224 | tf_op jit(solution)/shard_map/ppermute | solution.py:21
  42.6 9.8 %collective-permute-start.10 = (bf16[512,128]{1,0:T(8,128)(2,1)S(1)}, bf16[512,128]{1,0:T(8,128)(2,1)S(1)}, u32[]{:S(2)}, u32[]{:S(2)}) collective-permute-start(bf16[512,128]{1,0:T(8,128)(2,1)S(1)} %get-tuple-element.76.refs_0_), channel_id=1, source_target_pairs={{0,2},{2,0},{4,6},{6,4},{1,3},{3,1},{5,7},{7,5},{8,10},{10,8},{12,... | collective-permute-start | bytes 393224 | tf_op jit(solution)/shard_map/ppermute | solution.py:21
  42.6 7.6 %collective-permute-start.11 = (bf16[512,128]{1,0:T(8,128)(2,1)S(1)}, bf16[512,128]{1,0:T(8,128)(2,1)S(1)}, u32[]{:S(2)}, u32[]{:S(2)}) collective-permute-start(bf16[512,128]{1,0:T(8,128)(2,1)S(1)} %get-tuple-element.76.refs_0_), channel_id=1, source_target_pairs={{0,4},{2,6},{4,0},{6,2},{1,5},{3,7},{5,1},{7,3},{8,12},{10,14},{12... | collective-permute-start | bytes 393224 | tf_op jit(solution)/shard_map/ppermute | solution.py:21
  50.1 4.3 %collective-permute-start.13 = (bf16[512,128]{1,0:T(8,128)(2,1)S(1)}, bf16[512,128]{1,0:T(8,128)(2,1)S(1)}, u32[]{:S(2)}, u32[]{:S(2)}) collective-permute-start(bf16[512,128]{1,0:T(8,128)(2,1)S(1)} %get-tuple-element.74.refs_3_), channel_id=1, source_target_pairs={{0,2},{2,0},{4,6},{6,4},{1,3},{3,1},{5,7},{7,5},{8,10},{10,8},{12,... | collective-permute-start | bytes 393224 | tf_op jit(solution)/shard_map/ppermute | solution.py:21
  50.2 4.2 %collective-permute-start.12 = (bf16[512,128]{1,0:T(8,128)(2,1)S(1)}, bf16[512,128]{1,0:T(8,128)(2,1)S(1)}, u32[]{:S(2)}, u32[]{:S(2)}) collective-permute-start(bf16[512,128]{1,0:T(8,128)(2,1)S(1)} %collective-permute-done.11.refs_1_), channel_id=1, source_target_pairs={{0,2},{2,0},{4,6},{6,4},{1,3},{3,1},{5,7},{7,5},{8,10},{10,8},{12,... | collective-permute-start | bytes 393224 | tf_op jit(solution)/shard_map/ppermute | solution.py:21
  50.7 8.0 %collective-permute-start.14 = (bf16[512,128]{1,0:T(8,128)(2,1)S(1)}, bf16[512,128]{1,0:T(8,128)(2,1)S(1)}, u32[]{:S(2)}, u32[]{:S(2)}) collective-permute-start(bf16[512,128]{1,0:T(8,128)(2,1)S(1)} %get-tuple-element.74.refs_3_), channel_id=1, source_target_pairs={{0,4},{2,6},{4,0},{6,2},{1,5},{3,7},{5,1},{7,3},{8,12},{10,14},{12... | collective-permute-start | bytes 393224 | tf_op jit(solution)/shard_map/ppermute | solution.py:21
  62.2 9.2 %collective-permute-start.16 = (bf16[1024,128]{1,0:T(8,128)(2,1)S(1)}, bf16[1024,128]{1,0:T(8,128)(2,1)S(1)}, u32[]{:S(2)}, u32[]{:S(2)}) collective-permute-start(bf16[1024,128]{1,0:T(8,128)(2,1)S(1)} %get-tuple-element.42), channel_id=1, source_target_pairs={{0,8},{8,0},{16,24},{24,16},{1,9},{9,1},{17,25},{25,17},{2,10},{10... | collective-permute-start | bytes 786440 | tf_op jit(solution)/shard_map/ppermute | solution.py:21
  62.3 15.0 %collective-permute-start.18 = (bf16[1024,128]{1,0:T(8,128)(2,1)S(1)}, bf16[1024,128]{1,0:T(8,128)(2,1)S(1)}, u32[]{:S(2)}, u32[]{:S(2)}) collective-permute-start(bf16[1024,128]{1,0:T(8,128)(2,1)S(1)} %get-tuple-element.44), channel_id=1, source_target_pairs={{0,8},{8,0},{16,24},{24,16},{1,9},{9,1},{17,25},{25,17},{2,10},{10... | collective-permute-start | bytes 786440 | tf_op jit(solution)/shard_map/ppermute | solution.py:21
  71.5 8.5 %collective-permute-start.17 = (bf16[512,128]{1,0:T(8,128)(2,1)S(1)}, bf16[512,128]{1,0:T(8,128)(2,1)S(1)}, u32[]{:S(2)}, u32[]{:S(2)}) collective-permute-start(bf16[512,128]{1,0:T(8,128)(2,1)S(1)} %fusion.8), channel_id=1, source_target_pairs={{0,16},{8,24},{16,0},{24,8},{1,17},{9,25},{17,1},{25,9},{2,18},{10... | collective-permute-start | bytes 393224 | tf_op jit(solution)/shard_map/ppermute | solution.py:21
  77.3 8.1 %collective-permute-start.19 = (bf16[512,128]{1,0:T(8,128)(2,1)S(1)}, bf16[512,128]{1,0:T(8,128)(2,1)S(1)}, u32[]{:S(2)}, u32[]{:S(2)}) collective-permute-start(bf16[512,128]{1,0:T(8,128)(2,1)S(1)} %fusion.9), channel_id=1, source_target_pairs={{0,16},{8,24},{16,0},{24,8},{1,17},{9,25},{17,1},{25,9},{2,18},{10... | collective-permute-start | bytes 393224 | tf_op jit(solution)/shard_map/ppermute | solution.py:21
  80.3 6.9 %collective-permute-start.20 = (bf16[512,128]{1,0:T(8,128)(2,1)S(1)}, bf16[512,128]{1,0:T(8,128)(2,1)S(1)}, u32[]{:S(2)}, u32[]{:S(2)}) collective-permute-start(bf16[512,128]{1,0:T(8,128)(2,1)S(1)} %convert_element_type.111.refs_0_), channel_id=1, source_target_pairs={{0,2},{2,0},{4,6},{6,4},{1,3},{3,1},{5,7},{7,5},{8,10},{10,8},{12,... | collective-permute-start | bytes 393224 | tf_op jit(solution)/shard_map/ppermute | solution.py:21
  80.3 5.9 %collective-permute-start.21 = (bf16[512,128]{1,0:T(8,128)(2,1)S(1)}, bf16[512,128]{1,0:T(8,128)(2,1)S(1)}, u32[]{:S(2)}, u32[]{:S(2)}) collective-permute-start(bf16[512,128]{1,0:T(8,128)(2,1)S(1)} %convert_element_type.111.refs_0_), channel_id=1, source_target_pairs={{0,4},{2,6},{4,0},{6,2},{1,5},{3,7},{5,1},{7,3},{8,12},{10,14},{12... | collective-permute-start | bytes 393224 | tf_op jit(solution)/shard_map/ppermute | solution.py:21
  85.6 3.6 %collective-permute-start.23 = (bf16[512,128]{1,0:T(8,128)(2,1)S(1)}, bf16[512,128]{1,0:T(8,128)(2,1)S(1)}, u32[]{:S(2)}, u32[]{:S(2)}) collective-permute-start(bf16[512,128]{1,0:T(8,128)(2,1)S(1)} %get-tuple-element.72.refs_3_), channel_id=1, source_target_pairs={{0,2},{2,0},{4,6},{6,4},{1,3},{3,1},{5,7},{7,5},{8,10},{10,8},{12,... | collective-permute-start | bytes 393224 | tf_op jit(solution)/shard_map/ppermute | solution.py:21
  86.2 7.3 %collective-permute-start.24 = (bf16[512,128]{1,0:T(8,128)(2,1)S(1)}, bf16[512,128]{1,0:T(8,128)(2,1)S(1)}, u32[]{:S(2)}, u32[]{:S(2)}) collective-permute-start(bf16[512,128]{1,0:T(8,128)(2,1)S(1)} %get-tuple-element.72.refs_3_), channel_id=1, source_target_pairs={{0,4},{2,6},{4,0},{6,2},{1,5},{3,7},{5,1},{7,3},{8,12},{10,14},{12... | collective-permute-start | bytes 393224 | tf_op jit(solution)/shard_map/ppermute | solution.py:21
  97.0 13.8 %collective-permute-start.26 = (bf16[1024,128]{1,0:T(8,128)(2,1)S(1)}, bf16[1024,128]{1,0:T(8,128)(2,1)S(1)}, u32[]{:S(2)}, u32[]{:S(2)}) collective-permute-start(bf16[1024,128]{1,0:T(8,128)(2,1)S(1)} %get-tuple-element.50), channel_id=1, source_target_pairs={{0,8},{8,0},{16,24},{24,16},{1,9},{9,1},{17,25},{25,17},{2,10},{10... | collective-permute-start | bytes 786440 | tf_op jit(solution)/shard_map/ppermute | solution.py:21
  97.4 18.9 %collective-permute-start.28 = (bf16[1024,128]{1,0:T(8,128)(2,1)S(1)}, bf16[1024,128]{1,0:T(8,128)(2,1)S(1)}, u32[]{:S(2)}, u32[]{:S(2)}) collective-permute-start(bf16[1024,128]{1,0:T(8,128)(2,1)S(1)} %pad_maximum_fusion.1), channel_id=1, source_target_pairs={{0,16},{8,24},{16,0},{24,8},{1,17},{9,25},{17,1},{25,9},{2,18},{10... | collective-permute-start | bytes 786440 | tf_op jit(solution)/shard_map/ppermute | solution.py:21
  98.2 18.1 %collective-permute-start.27 = (bf16[1024,128]{1,0:T(8,128)(2,1)S(1)}, bf16[1024,128]{1,0:T(8,128)(2,1)S(1)}, u32[]{:S(2)}, u32[]{:S(2)}) collective-permute-start(bf16[1024,128]{1,0:T(8,128)(2,1)S(1)} %get-tuple-element.52), channel_id=1, source_target_pairs={{0,8},{8,0},{16,24},{24,16},{1,9},{9,1},{17,25},{25,17},{2,10},{10... | collective-permute-start | bytes 786440 | tf_op jit(solution)/shard_map/ppermute | solution.py:21
  117.8 6.6 %collective-permute-start.32 = (f32[3,128]{1,0:T(4,128)S(1)}, f32[3,128]{1,0:T(4,128)S(1)}, u32[]{:S(2)}, u32[]{:S(2)}) collective-permute-start(f32[3,128]{1,0:T(4,128)S(1)} %fusion.10), channel_id=1, source_target_pairs={{0,12},{2,14},{4,8},{6,10},{8,4},{10,6},{12,0},{14,2},{16,28},{18,... | collective-permute-start | bytes 4616 | tf_op jit(solution)/shard_map/ppermute | solution.py:21
  119.3 5.1 %collective-permute-start.31 = (f32[3,128]{1,0:T(4,128)S(1)}, f32[3,128]{1,0:T(4,128)S(1)}, u32[]{:S(2)}, u32[]{:S(2)}) collective-permute-start(f32[3,128]{1,0:T(4,128)S(1)} %fusion.10), channel_id=1, source_target_pairs={{0,8},{8,0},{16,24},{24,16},{1,9},{9,1},{17,25},{25,17},{2,10},{10... | collective-permute-start | bytes 4616 | tf_op jit(solution)/shard_map/ppermute | solution.py:21
  120.6 3.8 %collective-permute-start.30 = (f32[3,128]{1,0:T(4,128)S(1)}, f32[3,128]{1,0:T(4,128)S(1)}, u32[]{:S(2)}, u32[]{:S(2)}) collective-permute-start(f32[3,128]{1,0:T(4,128)S(1)} %fusion.10), channel_id=1, source_target_pairs={{0,4},{2,6},{4,0},{6,2},{1,5},{3,7},{5,1},{7,3},{8,12},{10,14},{12... | collective-permute-start | bytes 4616 | tf_op jit(solution)/shard_map/ppermute | solution.py:21
  121.4 14.2 %collective-permute-start.34 = (bf16[512,128]{1,0:T(8,128)(2,1)S(1)}, bf16[512,128]{1,0:T(8,128)(2,1)S(1)}, u32[]{:S(2)}, u32[]{:S(2)}) collective-permute-start(bf16[512,128]{1,0:T(8,128)(2,1)S(1)} %fusion.4), channel_id=1, source_target_pairs={{0,16},{8,24},{16,0},{24,8},{1,17},{9,25},{17,1},{25,9},{2,18},{10... | collective-permute-start | bytes 393224 | tf_op jit(solution)/shard_map/ppermute | solution.py:21
  122.1 13.5 %collective-permute-start.35 = (bf16[512,128]{1,0:T(8,128)(2,1)S(1)}, bf16[512,128]{1,0:T(8,128)(2,1)S(1)}, u32[]{:S(2)}, u32[]{:S(2)}) collective-permute-start(bf16[512,128]{1,0:T(8,128)(2,1)S(1)} %fusion.5), channel_id=1, source_target_pairs={{0,16},{8,24},{16,0},{24,8},{1,17},{9,25},{17,1},{25,9},{2,18},{10... | collective-permute-start | bytes 393224 | tf_op jit(solution)/shard_map/ppermute | solution.py:21
  124.4 12.3 %collective-permute-start.33 = (f32[3,128]{1,0:T(4,128)S(1)}, f32[3,128]{1,0:T(4,128)S(1)}, u32[]{:S(2)}, u32[]{:S(2)}) collective-permute-start(f32[3,128]{1,0:T(4,128)S(1)} %add_add_fusion), channel_id=1, source_target_pairs={{0,16},{8,24},{16,0},{24,8},{1,17},{9,25},{17,1},{25,9},{2,18},{10... | collective-permute-start | bytes 4616 | tf_op jit(solution)/shard_map/ppermute | solution.py:21
  (6 other events, 24.4 us)
